TPU v7x, 128 devices: a whole 4x4x4 slice. The times are simulated.
128 devices in a mesh: gx: 32 (over x, z, core), gy: 4 (over y).
Axes of the slice: x: 4, y: 4, z: 4, core: 2. Of those that a mesh axis runs over, the one named last changes fastest.
Arguments:
- velocity: float32 [3, 256, 256, 256], P(None, 'gx', 'gy'), may hold values from -10 to 10
Outputs:
- coefficient: float32 [256], P('gy')
- viscosity: float32 [256, 256, 256], P('gx', 'gy')
All inputs are finite; a program needn't handle non-finite values.
Results may differ from a plain program's by a relative error of at most 0.00002.
Values sent between devices are 32-bit elements; how exact they have to be, the bound alone decides.
A program may use at most 64 MiB of HBM per device.

v0:
```python
import jax
import jax.numpy as jnp
from jax import lax
from jax.sharding import PartitionSpec as P

step_stream = 2.0
step_wall = 0.5
step_span = 1.0
clip_high = 0.1
weights = (1.0, 1.0, 1.0, 2.0, 2.0, 2.0)
index_pairs = ((0, 0), (1, 1), (2, 2), (0, 1), (0, 2), (1, 2))


def padded_2(cells, sides, width, closed):
    for axis, dim in sides:
        count = lax.axis_size(axis)
        ends = count if closed else count - 1
        head = lax.slice_in_dim(cells, 0, width, axis=dim)
        tail = lax.slice_in_dim(cells, cells.shape[dim] - width, cells.shape[dim], axis=dim)
        cells = jnp.concatenate(
            [
                lax.ppermute(tail, axis, [(i, (i + 1) % count) for i in range(ends)]),
                cells,
                lax.ppermute(head, axis, [((i + 1) % count, i) for i in range(ends)]),
            ],
            axis=dim,
        )
    return cells


def copy_for_each(shard, axis):
    copies = jnp.broadcast_to(shard, (lax.axis_size(axis), *shard.shape))
    return lax.all_to_all(copies, axis, split_axis=0, concat_axis=0, tiled=True)


def over_copies(shard, axis):
    return copy_for_each(shard, axis).sum(axis=0)


def in_one(arrays, axis):
    ends = [0]
    for a in arrays:
        ends.append(ends[-1] + a.size)
    total = over_copies(jnp.concatenate([a.ravel() for a in arrays]), axis)
    return tuple((total[b:e].reshape(a.shape) for a, b, e in zip(arrays, ends, ends[1:])))


def strain_inner(padded):
    grad_stream = (padded[:, 2:, 1:-1] - padded[:, :-2, 1:-1]) * (0.5 / step_stream)
    grad_wall = (padded[:, 1:-1, 2:] - padded[:, 1:-1, :-2]) * (0.5 / step_wall)
    centre = padded[:, 1:-1, 1:-1]
    grad_span = (jnp.roll(centre, -1, 3) - jnp.roll(centre, 1, 3)) * (0.5 / step_span)
    gradients = (grad_stream, grad_wall, grad_span)
    return jnp.stack(
        [
            0.5 * (gradients[second][first] + gradients[first][second])
            for first, second in index_pairs
        ]
    )


def weight_column():
    return jnp.asarray(weights, jnp.float32).reshape(6, 1, 1, 1)


def magnitude(strain):
    return jnp.sqrt(2.0 * jnp.sum(weight_column() * strain * strain, axis=0))


def test_filter(field):
    smoothed = 0.25 * field[:, :-2] + 0.5 * field[:, 1:-1] + 0.25 * field[:, 2:]
    return 0.25 * jnp.roll(smoothed, 1, 3) + 0.5 * smoothed + 0.25 * jnp.roll(smoothed, -1, 3)


def plane_sums(velocity_pad, stress_pad, filtered_pad):
    strain_hat = strain_inner(filtered_pad)
    magnitude_hat = magnitude(strain_hat)
    row_values = velocity_pad[:, :, 1:-1]
    products = jnp.stack([row_values[first] * row_values[second] for first, second in index_pairs])
    product_hat = test_filter(products)
    centre = filtered_pad[:, 1:-1, 1:-1]
    leonard = product_hat - jnp.stack(
        [centre[first] * centre[second] for first, second in index_pairs]
    )
    trace_third = (leonard[0] + leonard[1] + leonard[2]) / 3.0
    leonard = jnp.concatenate([leonard[:3] - trace_third[None], leonard[3:]])
    model_tensor = 2.0 * (test_filter(stress_pad) - 4.0 * magnitude_hat[None] * strain_hat)
    numerator = jnp.sum(weight_column() * leonard * model_tensor, axis=(0, 1, 3))
    denominator = jnp.sum(weight_column() * model_tensor * model_tensor, axis=(0, 1, 3))
    return (numerator, denominator)


def local(velocity):
    wall_count = lax.axis_size("gy")
    wall_index = lax.axis_index("gy")
    padded = padded_2(velocity, (("gx", 1), ("gy", 2)), 2, True)
    row_ids = jnp.arange(padded.shape[2])
    interior = padded.shape[2] - 2 * 2
    low_wall = jnp.logical_and(wall_index == 0, row_ids < 2)
    high_wall = jnp.logical_and(wall_index == wall_count - 1, row_ids >= interior + 2)
    inside = jnp.logical_not(jnp.logical_or(low_wall, high_wall))
    wide_pad = jnp.where(inside[None, None, :, None], padded, 0.0)
    velocity_pad = wide_pad[:, 1:-1, 1:-1]
    strain_wide = strain_inner(wide_pad)
    strength_wide = magnitude(strain_wide)
    stress_pad = (strength_wide[None] * strain_wide)[:, :, 1:-1]
    strength = strength_wide[1:-1, 1:-1]
    filtered_pad = test_filter(wide_pad[:, :, 1:-1])
    numerator, denominator = plane_sums(velocity_pad, stress_pad, filtered_pad)
    numerator, denominator = in_one((numerator, denominator), "gx")
    raw_profile = jnp.clip(numerator / denominator, 0.0, clip_high)
    rim_values = padded_2(raw_profile, (("gy", 0),), 1, False)
    bottom = jnp.where(wall_index == 0, raw_profile[0], rim_values[0])
    top_edge = jnp.where(wall_index == wall_count - 1, raw_profile[-1], rim_values[-1])
    below_values = jnp.concatenate([bottom[None], raw_profile[:-1]])
    above_values = jnp.concatenate([raw_profile[1:], top_edge[None]])
    smooth = 0.25 * below_values + 0.5 * raw_profile + 0.25 * above_values
    return (smooth, smooth[None, :, None] * strength)


def solution(mesh):
    in_specs = (P(None, "gx", "gy", None),)
    out_specs = (P("gy"), P("gx", "gy", None))
    return jax.shard_map(local, mesh=mesh, in_specs=in_specs, out_specs=out_specs, check_vma=False)
```

profile of v0, /device:TPU:1, one launch (start us, length us, event | category | flops | bytes accessed | tf_op | source)
XLA Modules:
  0.0 89.4 jit_solution(1010127377330946981)
XLA Ops:
  0.6 1.3 %fusion.61 = (f32[3,2,64,256]{3,2,1,0:T(8,128)S(1)}, f32[3,2,64,256]{3,2,1,0:T(8,128)S(1)}) fusion(f32[3,8,64,256]{3,2,1,0:T(8,128)} %param.5), kind=kLoop, calls=%fused_computation.124 | loop fusion | bytes 1572864 | tf_op jit(solution)/shard_map/slice | solution.py:18
  2.0 3.1 %collective-permute-start = (f32[3,2,64,256]{3,2,1,0:T(8,128)S(1)}, f32[3,2,64,256]{3,2,1,0:T(8,128)S(1)}, u32[]{:S(2)}, u32[]{:S(2)}) collective-permute-start(f32[3,2,64,256]{3,2,1,0:T(8,128)S(1)} %get-tuple-element.34), channel_id=1, source_target_pairs={{0,4},{4,8},{8,12},{12,16},{16,20},{20,24},{24,28},{28,32},{32,36}... | collective-permute-start | bytes 1179656 | tf_op jit(solution)/shard_map/ppermute | solution.py:22
  5.0 4.7 %collective-permute-done = f32[3,2,64,256]{3,2,1,0:T(8,128)S(1)} collective-permute-done((f32[3,2,64,256]{3,2,1,0:T(8,128)S(1)}, f32[3,2,64,256]{3,2,1,0:T(8,128)S(1)}, u32[]{:S(2)}, u32[]{:S(2)}) %collective-permute-start) | collective-permute-done | bytes 393248 | tf_op jit(solution)/shard_map/ppermute | solution.py:22
  10.0 2.6 %collective-permute-done.1 = f32[3,2,64,256]{3,2,1,0:T(8,128)S(1)} collective-permute-done((f32[3,2,64,256]{3,2,1,0:T(8,128)S(1)}, f32[3,2,64,256]{3,2,1,0:T(8,128)S(1)}, u32[]{:S(2)}, u32[]{:S(2)}) %collective-permute-start.1) | collective-permute-done | bytes 393248 | tf_op jit(solution)/shard_map/ppermute | solution.py:24
  12.6 2.8 %collective-permute-start.3 = (f32[3,12,2,256]{3,2,1,0:T(2,128)S(1)}, f32[3,12,2,256]{3,2,1,0:T(2,128)S(1)}, u32[]{:S(2)}, u32[]{:S(2)}) collective-permute-start(f32[3,12,2,256]{3,2,1,0:T(2,128)S(1)} %get-tuple-element.22), channel_id=1, source_target_pairs={{1,0},{2,1},{3,2},{0,3},{5,4},{6,5},{7,6},{4,7},{9,8},{10,9},{11,1... | collective-permute-start | bytes 221192 | tf_op jit(solution)/shard_map/ppermute | solution.py:24
  15.5 1.4 %collective-permute-done.3 = f32[3,12,2,256]{3,2,1,0:T(2,128)S(1)} collective-permute-done((f32[3,12,2,256]{3,2,1,0:T(2,128)S(1)}, f32[3,12,2,256]{3,2,1,0:T(2,128)S(1)}, u32[]{:S(2)}, u32[]{:S(2)}) %collective-permute-start.3) | collective-permute-done | bytes 73760 | tf_op jit(solution)/shard_map/ppermute | solution.py:24
  16.8 3.0 %collective-permute-done.2 = f32[3,12,2,256]{3,2,1,0:T(2,128)S(1)} collective-permute-done((f32[3,12,2,256]{3,2,1,0:T(2,128)S(1)}, f32[3,12,2,256]{3,2,1,0:T(2,128)S(1)}, u32[]{:S(2)}, u32[]{:S(2)}) %collective-permute-start.2) | collective-permute-done | bytes 73760 | tf_op jit(solution)/shard_map/ppermute | solution.py:22
  21.9 1.4 %fusion.60 = (f32[3,10,66,1]{3,2,1,0:T(8,128)S(1)}, f32[3,10,66,1]{3,2,1,0:T(8,128)}) fusion(f32[3,10,66,256]{3,2,1,0:T(8,128)S(1)} %get-tuple-element.20), kind=kLoop, calls=%fused_computation.123 | loop fusion | bytes 31680 | tf_op jit(solution)/shard_map/jit(_roll_static)/slice | solution.py:72
  24.3 1.2 %fusion.52 = (f32[6,8,64,255]{3,2,1,0:T(8,128)S(1)}, f32[6,8,64,255]{3,2,1,0:T(8,128)S(1)}) fusion(f32[6,8,64,256]{3,2,1,0:T(8,128)S(1)} %fusion.4), kind=kLoop, calls=%fused_computation.115 | loop fusion | bytes 12533760 | tf_op jit(solution)/shard_map/jit(_roll_static)/slice | solution.py:72
  25.5 2.3 %fusion.53 = (f32[6,8,64,1]{3,2,1,0:T(8,128)}, f32[6,8,64,1]{3,2,1,0:T(8,128)}) fusion(f32[6,8,64,256]{3,2,1,0:T(8,128)S(1)} %fusion.4), kind=kLoop, calls=%fused_computation.116 | loop fusion | bytes 49152 | tf_op jit(solution)/shard_map/jit(_roll_static)/slice | solution.py:72
  27.8 2.6 %fusion.17 = f32[3,10,66,256]{3,2,1,0:T(8,128)S(1)} fusion(f32[3,10,66,255]{3,2,1,0:T(8,128)S(1)} %get-tuple-element.30, f32[3,10,66,1]{3,2,1,0:T(8,128)} %get-tuple-element.32, f32[3,10,66,1]{3,2,1,0:T(8,128)S(1)} %get-tuple-element.31, f32[3,10,66,255]{3,2,1,0:T(8,128)S(1)} %get-tuple-element.29, f32[3,10,66,256]{3,2,1,0:T(8,128)S(1)} %get-tuple-element.20), kind=kLoop, calls=%fused_computation.35 | loop fusion | flops 3548160 | bytes 8110080 | tf_op jit(solution)/shard_map/add | solution.py:72
  30.3 0.8 multiply_dynamic-update-slice_fusion.11
  31.2 2.2 %fusion.58 = (f32[3,8,64,255]{3,2,1,0:T(8,128)}, f32[3,8,64,255]{3,2,1,0:T(8,128)}) fusion(f32[3,10,66,256]{3,2,1,0:T(8,128)S(1)} %fusion.17), kind=kLoop, calls=%fused_computation.121 | loop fusion | bytes 6266880 | tf_op jit(solution)/shard_map/jit(_roll_static)/slice | solution.py:52
  33.4 1.4 %fusion.57 = (f32[3,8,64,1]{3,2,1,0:T(8,128)}, f32[3,8,64,1]{3,2,1,0:T(8,128)}) fusion(f32[3,10,66,256]{3,2,1,0:T(8,128)S(1)} %fusion.17), kind=kLoop, calls=%fused_computation.120 | loop fusion | bytes 24576 | tf_op jit(solution)/shard_map/jit(_roll_static)/slice | solution.py:52
  36.1 1.0 %fusion.18 = f32[3,10,66,256]{3,2,1,0:T(8,128)S(1)} fusion(f32[3,10,66,1]{3,2,1,0:T(8,128)S(1)} %get-tuple-element.15, f32[3,10,66,255]{3,2,1,0:T(8,128)S(1)} %get-tuple-element.17, f32[3,10,66,255]{3,2,1,0:T(8,128)S(1)} %get-tuple-element.16, f32[3,10,66,1]{3,2,1,0:T(8,128)S(1)} %get-tuple-element.14), kind=kLoop, calls=%fused_computation.38 | loop fusion | flops 2027520 | bytes 6082560 | tf_op jit(solution)/shard_map/mul | solution.py:52
  40.2 1.8 %fusion.51 = (f32[6,8,64,1]{3,2,1,0:T(8,128)S(1)}, f32[6,8,64,1]{3,2,1,0:T(8,128)}) fusion(f32[6,8,64,256]{3,2,1,0:T(8,128)S(1)} %fusion.2), kind=kLoop, calls=%fused_computation.114 | loop fusion | bytes 49152 | tf_op jit(solution)/shard_map/jit(_roll_static)/slice | solution.py:72
  42.0 3.0 %fusion.50 = (f32[6,8,64,255]{3,2,1,0:T(8,128)S(1)}, f32[6,8,64,255]{3,2,1,0:T(8,128)}) fusion(f32[6,8,64,256]{3,2,1,0:T(8,128)S(1)} %fusion.2), kind=kLoop, calls=%fused_computation.113 | loop fusion | bytes 12533760 | tf_op jit(solution)/shard_map/jit(_roll_static)/slice | solution.py:72
  45.0 0.8 multiply_dynamic-update-slice_fusion.10
  45.8 0.9 multiply_dynamic-update-slice_fusion.9
  46.7 0.9 multiply_dynamic-update-slice_fusion.8
  47.6 0.9 %multiply_dynamic-update-slice_fusion.7 = f32[6,8,64,256]{3,2,1,0:T(8,128)} fusion(f32[6,8,64,256]{3,2,1,0:T(8,128)} %multiply_dynamic-update-slice_fusion.8, f32[3,10,66,256]{3,2,1,0:T(8,128)S(1)} %fusion.17), kind=kLoop, calls=%fused_computation.97 | loop fusion | flops 131072 | bytes 1572864
  48.5 0.9 %multiply_dynamic-update-slice_fusion.6 = f32[6,8,64,256]{3,2,1,0:T(8,128)} fusion(f32[6,8,64,256]{3,2,1,0:T(8,128)} %multiply_dynamic-update-slice_fusion.7, f32[3,10,66,256]{3,2,1,0:T(8,128)S(1)} %fusion.17), kind=kLoop, calls=%fused_computation.96 | loop fusion | flops 131072 | bytes 1572864 | tf_op jit(solution)/shard_map/stack | solution.py:82
  49.4 3.8 %fusion.8 = f32[6,8,64,256]{3,2,1,0:T(8,128)S(1)} fusion(f32[6,8,64,256]{3,2,1,0:T(8,128)} %multiply_dynamic-update-slice_fusion.6, f32[6,8,64,255]{3,2,1,0:T(8,128)S(1)} %get-tuple-element.11, f32[6,8,64,1]{3,2,1,0:T(8,128)S(1)} %copy-done.2, f32[6,8,64,1]{3,2,1,0:T(8,128)S(1)} %copy-done.1, f32[6,8,64,255]{3,2,1,0:T(8,128)S(1)} %get-tuple-element.10, ...), kind=kLoop, calls=%fused_computation.17 | loop fusion | flops 10223616 | bytes 22020096 | tf_op jit(solution)/shard_map/sub | solution.py:82
  53.7 1.0 %copy-done.4 = f32[3,8,64,255]{3,2,1,0:T(8,128)S(1)} copy-done((f32[3,8,64,255]{3,2,1,0:T(8,128)S(1)}, f32[3,8,64,255]{3,2,1,0:T(8,128)}, u32[]{:S(2)}) %copy-start.4) | copy-done | bytes 1566744
  55.2 2.5 %slice_subtract_fusion.1 = (f32[3,8,64,256]{3,2,1,0:T(8,128)S(1)}, f32[3,8,64,256]{3,2,1,0:T(8,128)S(1)}, f32[3,8,64,256]{3,2,1,0:T(8,128)S(1)}) fusion(f32[3,10,66,256]{3,2,1,0:T(8,128)S(1)} %fusion.17, f32[3,8,64,255]{3,2,1,0:T(8,128)S(1)} %copy-done.4, f32[3,8,64,1]{3,2,1,0:T(8,128)} %get-tuple-element.23, f32[3,8,64,1]{3,2,1,0:T(8,128)} %get-tuple-element.24, ...), kind=kLoop, calls=%fused_computation.41 | loop fusion | flops 2752512 | bytes 14155776 | tf_op jit(solution)/shard_map/sub | solution.py:50
  58.7 1.2 %copy-done = f32[6,8,64,255]{3,2,1,0:T(8,128)S(1)} copy-done((f32[6,8,64,255]{3,2,1,0:T(8,128)S(1)}, f32[6,8,64,255]{3,2,1,0:T(8,128)}, u32[]{:S(2)}) %copy-start) | copy-done | bytes 3133464
  60.4 4.1 %fusion.10 = (f32[64]{0:T(128)S(1)}, f32[64]{0:T(128)S(1)}) fusion(f32[3,8,64,256]{3,2,1,0:T(8,128)S(1)} %get-tuple-element.9, f32[3,8,64,256]{3,2,1,0:T(8,128)S(1)} %get-tuple-element.8, f32[6]{0:T(128)S(1)} %copy-done.9, f32[6]{0:T(128)S(1)} %copy-done.11, f32[6,8,64,256]{3,2,1,0:T(8,128)S(1)} %fusion.34, f32[8,64,256]{2,1,0:T(8,128)S(1)} %sqrt_multiply_fusion, ...), kind=kLoop, calls=%fused_computation.21 | loop fusion | flops 17301376 | bytes 22544944 | tf_op jit(solution)/shard_map/reduce_sum | solution.py:88
  64.6 15.5 %all_to_all.6 = f32[32,1,128]{2,1,0:T(1,128)S(1)} all-to-all(f32[32,1,128]{2,1,0:T(1,128)S(1)} %broadcast_in_dim.28), channel_id=1, replica_groups=mesh['gx'=32,'gy'=4] {'gx'}, dimensions={0} | all-to-all | bytes 32768 | tf_op jit(solution)/shard_map/all_to_all | solution.py:33
  80.8 1.8 %collective-permute-start.4 = (f32[1]{0:T(128)}, f32[1]{0:T(128)}, u32[]{:S(2)}, u32[]{:S(2)}) collective-permute-start(f32[1]{0:T(128)} %get-tuple-element.37), channel_id=1, source_target_pairs={{0,1},{1,2},{2,3},{4,5},{5,6},{6,7},{8,9},{9,10},{10,11},{12,13},{... | collective-permute-start | bytes 20 | tf_op jit(solution)/shard_map/ppermute | solution.py:22
  82.6 1.3 %collective-permute-start.5 = (f32[1]{0:T(128)}, f32[1]{0:T(128)}, u32[]{:S(2)}, u32[]{:S(2)}) collective-permute-start(f32[1]{0:T(128)} %get-tuple-element.38), channel_id=1, source_target_pairs={{1,0},{2,1},{3,2},{5,4},{6,5},{7,6},{9,8},{10,9},{11,10},{13,12},{... | collective-permute-start | bytes 20 | tf_op jit(solution)/shard_map/ppermute | solution.py:24
  85.2 2.0 %collective-permute-done.5 = f32[1]{0:T(128)} collective-permute-done((f32[1]{0:T(128)}, f32[1]{0:T(128)}, u32[]{:S(2)}, u32[]{:S(2)}) %collective-permute-start.5) | collective-permute-done | bytes 36 | tf_op jit(solution)/shard_map/ppermute | solution.py:24
  88.5 0.9 %slice_multiply_fusion.7 = f32[8,64,256]{2,1,0:T(8,128)} fusion(f32[10,66,256]{2,1,0:T(8,128)S(1)} %copy-done.7, f32[64]{0:T(128)S(1)} %fusion.48), kind=kLoop, calls=%fused_computation.72 | loop fusion | flops 131072 | bytes 1048832 | tf_op jit(solution)/shard_map/mul | solution.py:118
  (69 shorter events, 11.0 us)
Async XLA Ops:
  0.6 9.2 %copy-start.8 = (f32[3,8,64,256]{3,2,1,0:T(8,128)S(1)}, f32[3,8,64,256]{3,2,1,0:T(8,128)}, u32[]{:S(2)}) copy-start(f32[3,8,64,256]{3,2,1,0:T(8,128)} %param.5) | copy-start | bytes 4718596
  2.0 7.8 %collective-permute-start = (f32[3,2,64,256]{3,2,1,0:T(8,128)S(1)}, f32[3,2,64,256]{3,2,1,0:T(8,128)S(1)}, u32[]{:S(2)}, u32[]{:S(2)}) collective-permute-start(f32[3,2,64,256]{3,2,1,0:T(8,128)S(1)} %get-tuple-element.34), channel_id=1, source_target_pairs={{0,4},{4,8},{8,12},{12,16},{16,20},{20,24},{24,28},{28,32},{32,36}... | collective-permute-start | bytes 1179656 | tf_op jit(solution)/shard_map/ppermute | solution.py:22
  5.0 7.5 %collective-permute-start.1 = (f32[3,2,64,256]{3,2,1,0:T(8,128)S(1)}, f32[3,2,64,256]{3,2,1,0:T(8,128)S(1)}, u32[]{:S(2)}, u32[]{:S(2)}) collective-permute-start(f32[3,2,64,256]{3,2,1,0:T(8,128)S(1)} %get-tuple-element.33), channel_id=1, source_target_pairs={{4,0},{8,4},{12,8},{16,12},{20,16},{24,20},{28,24},{32,28},{36,32}... | collective-permute-start | bytes 1179656 | tf_op jit(solution)/shard_map/ppermute | solution.py:24
  12.6 4.2 %collective-permute-start.3 = (f32[3,12,2,256]{3,2,1,0:T(2,128)S(1)}, f32[3,12,2,256]{3,2,1,0:T(2,128)S(1)}, u32[]{:S(2)}, u32[]{:S(2)}) collective-permute-start(f32[3,12,2,256]{3,2,1,0:T(2,128)S(1)} %get-tuple-element.22), channel_id=1, source_target_pairs={{1,0},{2,1},{3,2},{0,3},{5,4},{6,5},{7,6},{4,7},{9,8},{10,9},{11,1... | collective-permute-start | bytes 221192 | tf_op jit(solution)/shard_map/ppermute | solution.py:24
  15.4 4.4 %collective-permute-start.2 = (f32[3,12,2,256]{3,2,1,0:T(2,128)S(1)}, f32[3,12,2,256]{3,2,1,0:T(2,128)S(1)}, u32[]{:S(2)}, u32[]{:S(2)}) collective-permute-start(f32[3,12,2,256]{3,2,1,0:T(2,128)S(1)} %get-tuple-element.21), channel_id=1, source_target_pairs={{0,1},{1,2},{2,3},{3,0},{4,5},{5,6},{6,7},{7,4},{8,9},{9,10},{10,1... | collective-permute-start | bytes 221192 | tf_op jit(solution)/shard_map/ppermute | solution.py:22
  37.1 0.7 copy-start.9
  38.6 0.9 %copy-start.6 = (f32[10,66,256]{2,1,0:T(8,128)}, f32[10,66,256]{2,1,0:T(8,128)S(1)}, u32[]{:S(2)}) copy-start(f32[10,66,256]{2,1,0:T(8,128)S(1)} %multiply_sqrt_fusion) | copy-start | bytes 2027524
  45.8 3.5 %copy-start.1 = (f32[6,8,64,1]{3,2,1,0:T(8,128)S(1)}, f32[6,8,64,1]{3,2,1,0:T(8,128)}, u32[]{:S(2)}) copy-start(f32[6,8,64,1]{3,2,1,0:T(8,128)} %get-tuple-element.12) | copy-start | bytes 36868
  45.8 3.5 %copy-start.2 = (f32[6,8,64,1]{3,2,1,0:T(8,128)S(1)}, f32[6,8,64,1]{3,2,1,0:T(8,128)}, u32[]{:S(2)}) copy-start(f32[6,8,64,1]{3,2,1,0:T(8,128)} %get-tuple-element.13) | copy-start | bytes 36868
  53.3 1.4 %copy-start.4 = (f32[3,8,64,255]{3,2,1,0:T(8,128)S(1)}, f32[3,8,64,255]{3,2,1,0:T(8,128)}, u32[]{:S(2)}) copy-start(f32[3,8,64,255]{3,2,1,0:T(8,128)} %get-tuple-element.25) | copy-start | bytes 4700164
  53.3 1.9 %copy-start.5 = (f32[3,8,64,255]{3,2,1,0:T(8,128)S(1)}, f32[3,8,64,255]{3,2,1,0:T(8,128)}, u32[]{:S(2)}) copy-start(f32[3,8,64,255]{3,2,1,0:T(8,128)} %get-tuple-element.26) | copy-start | bytes 4700164
  58.0 1.9 %copy-start = (f32[6,8,64,255]{3,2,1,0:T(8,128)S(1)}, f32[6,8,64,255]{3,2,1,0:T(8,128)}, u32[]{:S(2)}) copy-start(f32[6,8,64,255]{3,2,1,0:T(8,128)} %get-tuple-element.5) | copy-start | bytes 9400324
  58.0 2.3 %copy-start.3 = (f32[6,8,64,1]{3,2,1,0:T(8,128)S(1)}, f32[6,8,64,1]{3,2,1,0:T(8,128)}, u32[]{:S(2)}) copy-start(f32[6,8,64,1]{3,2,1,0:T(8,128)} %get-tuple-element.7) | copy-start | bytes 36868
  58.0 2.3 %copy-start.11 = (f32[6]{0:T(128)S(1)}, f32[6]{0:T(128)}, u32[]{:S(2)}) copy-start(f32[6]{0:T(128)} %constant.6) | copy-start | bytes 76
  60.4 28.2 %copy-start.7 = (f32[10,66,256]{2,1,0:T(8,128)S(1)}, f32[10,66,256]{2,1,0:T(8,128)}, u32[]{:S(2)}) copy-start(f32[10,66,256]{2,1,0:T(8,128)} %copy-done.6) | copy-start | bytes 2027524
  80.8 3.1 %collective-permute-start.4 = (f32[1]{0:T(128)}, f32[1]{0:T(128)}, u32[]{:S(2)}, u32[]{:S(2)}) collective-permute-start(f32[1]{0:T(128)} %get-tuple-element.37), channel_id=1, source_target_pairs={{0,1},{1,2},{2,3},{4,5},{5,6},{6,7},{8,9},{9,10},{10,11},{12,13},{... | collective-permute-start | bytes 20 | tf_op jit(solution)/shard_map/ppermute | solution.py:22
  82.6 4.5 %collective-permute-start.5 = (f32[1]{0:T(128)}, f32[1]{0:T(128)}, u32[]{:S(2)}, u32[]{:S(2)}) collective-permute-start(f32[1]{0:T(128)} %get-tuple-element.38), channel_id=1, source_target_pairs={{1,0},{2,1},{3,2},{5,4},{6,5},{7,6},{9,8},{10,9},{11,10},{13,12},{... | collective-permute-start | bytes 20 | tf_op jit(solution)/shard_map/ppermute | solution.py:24
  88.5 0.9 %copy-start.10 = (f32[64]{0:T(128)}, f32[64]{0:T(128)S(1)}, u32[]{:S(2)}) copy-start(f32[64]{0:T(128)S(1)} %fusion.48) | copy-start | bytes 772
where the time goes:
time: 90 us; the launch traced here: 89.4 us
  other arithmetic  26.4 us (29%)
  local copies, waits for them, and re-layouts  21.4 us (24%)
  blocking collectives  15.5 us (17%)
  waiting for transfers between devices  13.7 us (15%)
  starting transfers between devices  8.98 us (10%)
  between operations  3.6 us (4%)
    all_to_all x1, blocking collectives, copy_for_each(): return lax.all_to_all(copies, axis, split_axis=0, concat_axis=0, tiled=True)  15.5 us
    slice x6, local copies, waits for them, and re-layouts, test_filter(): jnp.roll(smoothed, -1, 3)  10.3 us
    ppermute x3, waiting for transfers between devices, padded_2(): lax.ppermute(tail, axis, [(i, (i + 1) % count) for i in range(ends)])  7.73 us
    ppermute x3, waiting for transfers between devices, padded_2(): lax.ppermute(head, axis, [((i + 1) % count, i) for i in range(ends)])  5.93 us
    unnamed x20, other arithmetic  5.41 us
    ppermute x3, starting transfers between devices, padded_2(): lax.ppermute(tail, axis, [(i, (i + 1) % count) for i in range(ends)])  4.89 us
    slice x4, local copies, waits for them, and re-layouts, strain_inner(): jnp.roll(centre, 1, 3)  4.78 us
    unnamed x26, local copies, waits for them, and re-layouts  4.18 us
  transfers between devices with their start and end apart: 6, of which 5 were waited for; matrix products, arithmetic and copies ran while one was open for 0% of the time, Pallas kernels for 0%

commit v1 on v0

v1 whole, which is shorter than its diff:
```python
import functools

import jax
import jax.numpy as jnp
from jax import lax
from jax.experimental import pallas as pl
from jax.experimental.pallas import tpu as pltpu
from jax.sharding import PartitionSpec as P

F32 = jnp.float32
MESH = pl.DeviceIdType.MESH
XL = 8
YL = 64
ZL = 256
HALF = 128
CHUNKS = 4
CHUNK = YL // CHUNKS
clip_high = 0.1


def next_odd(a):
    return pltpu.roll(a, HALF - 1, 1)


def prev_even(a):
    return pltpu.roll(a, 1, 1)


def span_diff(even, odd):
    return odd - prev_even(odd), next_odd(even) - even


def span_sum(even, odd):
    pair_even = even + odd
    pair_odd = odd + next_odd(even)
    return pair_even + prev_even(pair_odd), pair_even + pair_odd


def gradients(ref, row, start, lead):
    stream = [[None] * 2 for _ in range(3)]
    wall = [[None] * 2 for _ in range(3)]
    span = [None] * 3
    middle = [[None] * 2 for _ in range(3)]
    sides = [[None] * 2 for _ in range(3)]
    for c in range(3):
        for h in range(2):
            above = ref[row + 1, c, h, start : start + 8, :]
            below = ref[row - 1, c, h, start : start + 8, :]
            stream[c][h] = above - below
            sides[c][h] = above + below if lead else None
            wall[c][h] = (
                ref[row, c, h, start + 1 : start + 9, :] - ref[row, c, h, start - 1 : start + 7, :]
            )
            middle[c][h] = ref[row, c, h, start : start + 8, :]
        span[c] = span_diff(middle[c][0], middle[c][1])
    return stream, wall, span, middle, sides


def tensor(stream, wall, span, h):
    d0, d1, d2 = stream[0][h], wall[1][h], span[2][h]
    t01 = wall[0][h] + 0.25 * stream[1][h]
    t02 = span[0][h] + 0.5 * stream[2][h]
    t12 = span[1][h] + 2.0 * wall[2][h]
    square = t01 * t01 + 0.25 * (0.5 * (d0 * d0) + t02 * t02 + t12 * t12)
    square = square + (2.0 * (d1 * d1) + 0.5 * (d2 * d2))
    return (d0, d1, d2, t01, t02, t12), jnp.sqrt(square)


def strain_unit(w, st, vf, sr, xi, k):
    r = 6 + 8 * k
    stream, wall, span, middle, sides = gradients(w, xi + 1, r, True)
    for h in range(2):
        parts, mag = tensor(stream, wall, span, h)
        quarter, half = 0.25 * mag, 0.5 * mag
        factors = (quarter, mag, half, half, quarter, quarter)
        for p in range(6):
            st[xi, p, h, 8 * k : 8 * k + 8, :] = factors[p] * parts[p]
        sr[xi, h, 8 * k : 8 * k + 8, :] = mag
    for c in range(3):
        smooth = [sides[c][h] + (middle[c][h] + middle[c][h]) for h in range(2)]
        both = span_sum(smooth[0], smooth[1])
        for h in range(2):
            vf[xi, c, h, 8 + 8 * k : 16 + 8 * k, :] = 0.25 * both[h]


def sums_unit(w, st, vf, acc, xo, k):
    r = 6 + 8 * k
    j = 8 * k
    stream, wall, span, middle, _ = gradients(vf, xo + 1, 8 + j, False)
    model = [[None] * 6 for _ in range(2)]
    leonard = [[None] * 6 for _ in range(2)]
    for p in range(6):
        line = []
        for h in range(2):
            mid = st[xo + 1, p, h, j : j + 8, :]
            line.append(
                st[xo, p, h, j : j + 8, :] + st[xo + 2, p, h, j : j + 8, :] + (mid + mid)
            )
        both = span_sum(line[0], line[1])
        for h in range(2):
            model[h][p] = both[h]
    for h in range(2):
        parts, mag = tensor(stream, wall, span, h)
        twice, four = 2.0 * mag, 4.0 * mag
        factors = (mag, four, twice, twice, mag, mag)
        for p in range(6):
            model[h][p] = model[h][p] - factors[p] * parts[p]
    rows = [
        [[w[xo + 1 + i, c, h, r : r + 8, :] for h in range(2)] for c in range(3)] for i in range(3)
    ]
    for p, (a, b) in enumerate(((0, 0), (1, 1), (2, 2), (0, 1), (0, 2), (1, 2))):
        line = []
        for h in range(2):
            mid = rows[1][a][h] * rows[1][b][h]
            line.append(
                rows[0][a][h] * rows[0][b][h] + rows[2][a][h] * rows[2][b][h] + (mid + mid)
            )
        both = span_sum(line[0], line[1])
        for h in range(2):
            leonard[h][p] = both[h] - middle[a][h] * middle[b][h]
    num = den = None
    for h in range(2):
        lo, mo = leonard[h], model[h]
        third = (lo[0] + lo[1] + lo[2]) * (1.0 / 3.0)
        n_diag = (lo[0] - third) * mo[0] + (lo[1] - third) * mo[1] + (lo[2] - third) * mo[2]
        n_off = lo[3] * mo[3] + lo[4] * mo[4] + lo[5] * mo[5]
        d_diag = mo[0] * mo[0] + mo[1] * mo[1] + mo[2] * mo[2]
        d_off = mo[3] * mo[3] + mo[4] * mo[4] + mo[5] * mo[5]
        n = n_diag + (n_off + n_off)
        d = d_diag + (d_off + d_off)
        num = n if num is None else num + n
        den = d if den is None else den + d
    acc[0, j : j + 8, :] += num
    acc[1, j : j + 8, :] += den


def over_rows(base, count, body):
    def step(i, carry):
        body(base + i)
        return carry

    lax.fori_loop(0, count, step, 0)


def main_kernel(
    nx, ny,
    vel, strength, cexp, crow,
    nat, w, st, vf, sr, acc, msg, gath,
    in_sem, slow_send, slow_recv, fast_send, fast_recv, wall_send, wall_recv,
    corner_send, corner_recv, sum_send, sum_recv,
):
    mx = lax.axis_index("gx")
    my = lax.axis_index("gy")
    core = lax.rem(mx, 2)
    right = lax.rem(mx + 1, nx)
    left = lax.rem(mx + nx - 1, nx)
    slow = core * right + (1 - core) * left
    fast = core * left + (1 - core) * right
    has_low = my > 0
    has_high = my < ny - 1

    barrier = pltpu.get_barrier_semaphore()
    for p in range(1, nx):
        pl.semaphore_signal(
            barrier, inc=1, device_id=(lax.rem(mx + p, nx), my), device_id_type=MESH
        )

    @pl.when(has_low)
    def _():
        pl.semaphore_signal(barrier, inc=1, device_id=(mx, my - 1), device_id_type=MESH)

    @pl.when(has_high)
    def _():
        pl.semaphore_signal(barrier, inc=1, device_id=(mx, my + 1), device_id_type=MESH)

    loads = [
        pltpu.make_async_copy(
            vel.at[:, 2 * g : 2 * g + 2], nat.at[:, 2 * g : 2 * g + 2], in_sem.at[g]
        )
        for g in range(4)
    ]
    for load in loads:
        load.start()

    def clear(first, count):
        def body(x):
            for c in range(3):
                for h in range(2):
                    w[x, c, h, first : first + count, :] = jnp.zeros((count, HALF), F32)

        return lambda: over_rows(0, 12, body)

    clear(0, 6)()
    clear(74, 6)()
    pl.when(jnp.logical_not(has_low))(clear(6, 2))
    pl.when(jnp.logical_not(has_high))(clear(72, 2))
    acc[...] = jnp.zeros_like(acc)

    lane = lax.broadcasted_iota(jnp.int32, (8, HALF), 1)
    sub = lax.broadcasted_iota(jnp.int32, (8, HALF), 0)
    low_lane = lane < 64
    pick_left = lax.rem(lane, 64) * 2 + lax.div(lane, 64)
    pick_right = lax.rem(lane, 64) * 2 + (1 - lax.div(lane, 64))

    def split(x):
        for c in range(3):
            for m in range(8):
                a = nat[c, x, 8 * m : 8 * m + 8, 0:128]
                b = nat[c, x, 8 * m : 8 * m + 8, 128:256]
                a = jnp.take_along_axis(a, pick_left, axis=1)
                b = jnp.take_along_axis(b, pick_right, axis=1)
                w[x + 2, c, 0, 8 + 8 * m : 16 + 8 * m, :] = jnp.where(low_lane, a, b)
                w[x + 2, c, 1, 8 + 8 * m : 16 + 8 * m, :] = pltpu.roll(
                    jnp.where(low_lane, b, a), 64, 1
                )

    for g in range(4):
        loads[g].wait()
        over_rows(2 * g, 2, split)

    pl.semaphore_wait(
        barrier, nx - 1 + has_low.astype(jnp.int32) + has_high.astype(jnp.int32)
    )

    def edge(src, dst, rows_from, rows_to, count, sems, to):
        return pltpu.make_async_remote_copy(
            src_ref=w.at[pl.ds(src[0], src[1]), :, :, rows_from : rows_from + count, :],
            dst_ref=w.at[pl.ds(dst[0], dst[1]), :, :, rows_to : rows_to + count, :],
            send_sem=sems[0],
            recv_sem=sems[1],
            device_id=to,
            device_id_type=MESH,
        )

    slow_src, slow_dst = 2 + 6 * core, 10 - 10 * core
    fast_src, fast_dst = 8 - 6 * core, 10 * core
    slow_copies = [
        edge(
            (slow_src, 2), (slow_dst, 2), 8 + CHUNK * c, 8 + CHUNK * c, CHUNK,
            (slow_send.at[c], slow_recv.at[c]), (slow, my),
        )
        for c in range(CHUNKS)
    ]
    fast_copy = edge((fast_src, 2), (fast_dst, 2), 8, 8, YL, (fast_send, fast_recv), (fast, my))
    to_low = edge((2, 8), (2, 8), 8, 72, 2, (wall_send.at[0], wall_recv.at[0]), (mx, my - 1))
    to_high = edge((2, 8), (2, 8), 70, 6, 2, (wall_send.at[1], wall_recv.at[1]), (mx, my + 1))
    slow_copies[0].start()
    pl.when(has_low)(to_low.start)
    pl.when(has_high)(to_high.start)
    fast_copy.start()
    for c in range(1, CHUNKS):
        slow_copies[c].start()

    def strains(ks):
        def body(xi):
            for k in ks:
                strain_unit(w, st, vf, sr, xi, k)

        return body

    def sums(ks):
        def body(xo):
            for k in ks:
                sums_unit(w, st, vf, acc, xo, k)

        return body

    fast_first = 8 - 8 * core
    near_first = 2 - 2 * core
    over_rows(2, 6, strains(range(1, 8)))
    fast_copy.wait_recv()
    over_rows(fast_first, 2, strains(range(1, 8)))
    over_rows(near_first, 6, sums(range(2, 7)))

    corner_slow_low = edge(
        (slow_src, 2), (slow_dst, 2), 6, 6, 2, (corner_send.at[0], corner_recv.at[0]), (slow, my)
    )
    corner_slow_high = edge(
        (slow_src, 2), (slow_dst, 2), 72, 72, 2, (corner_send.at[1], corner_recv.at[1]), (slow, my)
    )
    corner_fast_low = edge(
        (fast_src, 2), (fast_dst, 2), 6, 6, 2, (corner_send.at[2], corner_recv.at[2]), (fast, my)
    )
    corner_fast_high = edge(
        (fast_src, 2), (fast_dst, 2), 72, 72, 2, (corner_send.at[3], corner_recv.at[3]), (fast, my)
    )

    @pl.when(has_low)
    def _():
        to_high.wait_recv()
        corner_slow_low.start()
        corner_fast_low.start()

    @pl.when(has_high)
    def _():
        to_low.wait_recv()
        corner_slow_high.start()
        corner_fast_high.start()

    over_rows(2, 6, strains((0, 8)))
    pl.when(has_low)(corner_fast_low.wait_recv)
    pl.when(has_high)(corner_fast_high.wait_recv)
    over_rows(fast_first, 2, strains((0, 8)))
    over_rows(near_first, 6, sums((0, 1, 7, 8)))

    slow_first = 8 * core
    far_first = 6 * core
    groups = (((0, 1), (0,)), ((2, 3), (1, 2)), ((4, 5), (3, 4)), ((6, 7, 8), (5, 6, 7, 8)))
    for c in range(CHUNKS):
        slow_copies[c].wait_recv()
        if c == 0:
            pl.when(has_low)(corner_slow_low.wait_recv)
        if c == CHUNKS - 1:
            pl.when(has_high)(corner_slow_high.wait_recv)
        over_rows(slow_first, 2, strains(groups[c][0]))
        over_rows(far_first, 2, sums(groups[c][1]))

    packs = []
    for q in range(2):
        table = jnp.zeros((8, HALF), F32)
        for k in range(9):
            column = jnp.sum(acc[q, 8 * k : 8 * k + 8, :], axis=1, keepdims=True)
            table = jnp.where(lane == k, column, table)
        spread = pltpu.roll(table, 0, 1, stride=16, stride_axis=0)
        packs.append(jnp.sum(spread, axis=0, keepdims=True))
    for q in range(2):
        msg[q : q + 1, :] = packs[q]
        gath[mx, q : q + 1, :] = packs[q]

    def gather_copy(to):
        return pltpu.make_async_remote_copy(
            src_ref=msg,
            dst_ref=gath.at[mx],
            send_sem=sum_send,
            recv_sem=sum_recv,
            device_id=(to, my),
            device_id_type=MESH,
        )

    for p in range(1, nx):
        gather_copy(lax.rem(mx + p, nx)).start()

    even_lane = lax.rem(lane, 2) == 0
    pick_low = lax.div(lane, 2)
    pick_high = pick_low + 64

    def join(x):
        for m in range(8):
            even = sr[x + 1, 0, 8 * m + 2 : 8 * m + 10, :]
            odd = sr[x + 1, 1, 8 * m + 2 : 8 * m + 10, :]
            for side, pick in enumerate((pick_low, pick_high)):
                strength[x, 8 * m : 8 * m + 8, 128 * side : 128 * side + 128] = jnp.where(
                    even_lane,
                    jnp.take_along_axis(even, pick, axis=1),
                    jnp.take_along_axis(odd, pick, axis=1),
                )

    over_rows(0, XL, join)

    everyone = pltpu.make_async_remote_copy(
        src_ref=gath.at[0 : nx - 1],
        dst_ref=gath.at[0 : nx - 1],
        send_sem=sum_send,
        recv_sem=sum_recv,
        device_id=(right, my),
        device_id_type=MESH,
    )
    everyone.wait_recv()
    terms = [gath[i] for i in range(nx)]
    while len(terms) > 1:
        terms = [a + b for a, b in zip(terms[::2], terms[1::2])]
    total = terms[0]
    raw = jnp.clip(0.5 * (total[0:1, :] / total[1:2, :]), 0.0, clip_high)
    raw = jnp.broadcast_to(raw, (8, HALF))
    below = jnp.where(lane < 16, pltpu.roll(raw, 17, 1), pltpu.roll(raw, 16, 1))
    above = jnp.where(lane >= 112, pltpu.roll(raw, 111, 1), pltpu.roll(raw, 112, 1))
    below = jnp.where(jnp.logical_and(lane == 32, jnp.logical_not(has_low)), raw, below)
    above = jnp.where(jnp.logical_and(lane == 24, jnp.logical_not(has_high)), raw, above)
    smooth = 0.25 * below + 0.5 * raw + 0.25 * above
    row = lane + 2
    crow[...] = jnp.take_along_axis(
        smooth, lax.rem(16 * lax.rem(row, 8) + lax.div(row, 8), HALF), axis=1
    )
    row = 8 * lane + sub + 2
    cexp[...] = jnp.take_along_axis(
        smooth, lax.rem(16 * lax.rem(row, 8) + lax.div(row, 8), HALF), axis=1
    )

    for copy in slow_copies:
        copy.wait_send()
    fast_copy.wait_send()

    @pl.when(has_low)
    def _():
        to_low.wait_send()
        corner_slow_low.wait_send()
        corner_fast_low.wait_send()

    @pl.when(has_high)
    def _():
        to_high.wait_send()
        corner_slow_high.wait_send()
        corner_fast_high.wait_send()

    everyone.wait_send()


def scale_kernel(strength, cexp, crow, coefficient, viscosity):
    coefficient[...] = crow[0:1, 0:YL]
    for m in range(8):
        column = cexp[:, m : m + 1]
        for x in range(XL):
            for side in range(2):
                at = (x, slice(8 * m, 8 * m + 8), slice(128 * side, 128 * side + 128))
                viscosity[at] = strength[at] * column


def local(nx, ny, velocity):
    vmem = pl.BlockSpec(memory_space=pltpu.VMEM)
    dma = pltpu.SemaphoreType.DMA
    strength, cexp, crow = pl.pallas_call(
        functools.partial(main_kernel, nx, ny),
        out_shape=(
            jax.ShapeDtypeStruct((XL, YL, ZL), F32),
            jax.ShapeDtypeStruct((8, HALF), F32),
            jax.ShapeDtypeStruct((8, HALF), F32),
        ),
        in_specs=[pl.BlockSpec(memory_space=pl.ANY)],
        out_specs=(vmem, vmem, vmem),
        scratch_shapes=[
            pltpu.VMEM((3, XL, YL, ZL), F32),
            pltpu.VMEM((12, 3, 2, 80, HALF), F32),
            pltpu.VMEM((10, 6, 2, 72, HALF), F32),
            pltpu.VMEM((10, 3, 2, 88, HALF), F32),
            pltpu.VMEM((10, 2, 72, HALF), F32),
            pltpu.VMEM((2, 72, HALF), F32),
            pltpu.VMEM((2, HALF), F32),
            pltpu.VMEM((nx, 2, HALF), F32),
            dma((4,)),
            dma((CHUNKS,)),
            dma((CHUNKS,)),
            dma,
            dma,
            dma((2,)),
            dma((2,)),
            dma((4,)),
            dma((4,)),
            dma,
            dma,
        ],
        compiler_params=pltpu.CompilerParams(collective_id=0, has_side_effects=True),
        name="germano",
    )(velocity)
    coefficient, viscosity = pl.pallas_call(
        scale_kernel,
        out_shape=(
            jax.ShapeDtypeStruct((1, YL), F32),
            jax.ShapeDtypeStruct((XL, YL, ZL), F32),
        ),
        in_specs=[vmem, vmem, vmem],
        out_specs=(vmem, vmem),
        name="scale",
    )(strength, cexp, crow)
    return coefficient.reshape(YL), viscosity


def solution(mesh):
    nx, ny = mesh.shape["gx"], mesh.shape["gy"]
    return jax.shard_map(
        functools.partial(local, nx, ny),
        mesh=mesh,
        in_specs=(P(None, "gx", "gy", None),),
        out_specs=(P("gy"), P("gx", "gy", None)),
        check_vma=False,
    )
```

time: 90 us -> 26.6 us (0.30)
  other arithmetic: 26.4 us -> 0 us
  Pallas kernels: 0 us -> 25.8 us
  local copies, waits for them, and re-layouts: 21.4 us -> 0 us
  blocking collectives: 15.5 us -> 0 us
  waiting for transfers between devices: 13.7 us -> 0 us
  starting transfers between devices: 8.98 us -> 0 us
  between operations: 3.6 us -> 0.64 us
    pallas_call x0 -> x2, Pallas kernels: none -> 25.8 us  [the longest x1 23.9 us: local(): pl.pallas_call(functools.partial(main_kernel, nx, ny), out_shape=(jax.Sha...]
    slice x14 -> x0, local copies, waits for them, and re-layouts: 17.1 us -> none  [the longest x6 10.3 us: test_filter(): jnp.roll(smoothed, -1, 3)]
    all_to_all x1 -> x0, blocking collectives: 15.5 us -> none  [copy_for_each(): return lax.all_to_all(copies, axis, split_axis=0, concat_axis=0, tiled=True)]
    ppermute x6 -> x0, waiting for transfers between devices: 13.7 us -> none  [the longest x3 7.73 us: padded_2(): lax.ppermute(tail, axis, [(i, (i + 1) % count) for i in range(ends)])]
    ppermute x6 -> x0, starting transfers between devices: 8.98 us -> none  [the longest x3 4.89 us: padded_2(): lax.ppermute(tail, axis, [(i, (i + 1) % count) for i in range(ends)])]
    sub x5 -> x0, other arithmetic: 7.67 us -> none  [the longest x1 3.78 us: plane_sums(): product_hat - jnp.stack([centre[first] * centre[second] for first, second...]
    unnamed x20 -> x0, other arithmetic: 5.41 us -> none
    reduce_sum x4 -> x0, other arithmetic: 5.15 us -> none  [the longest x1 4.14 us: plane_sums(): jnp.sum(weight_column() * leonard * model_tensor, axis=(0, 1, 3))]
  transfers between devices with their start and end apart: 6 -> 0, of which waited for: 5 -> 0; matrix products, arithmetic and copies ran while one was open for 0% -> 0% of each run, Pallas kernels for 0% -> 0%
where the time goes in v1:
time: 26.6 us; the launch traced here: 26.5 us
  Pallas kernels  25.8 us (97%)
  between operations  0.64 us (2%)
    pallas_call x1, Pallas kernels, local(): pl.pallas_call(functools.partial(main_kernel, nx, ny), out_shape=(jax.Sha...  23.9 us
    pallas_call x1, Pallas kernels, local(): pl.pallas_call(scale_kernel, out_shape=(jax.ShapeDtypeStruct((1, YL), F32...  1.95 us

profile of v1, /device:TPU:1, one launch (start us, length us, event | category | flops | bytes accessed | tf_op | source)
XLA Modules:
  0.0 26.5 jit_solution(3039337634156404224)
XLA Ops:
  0.6 23.9 %germano.1 = (f32[8,64,256]{2,1,0:T(8,128)}, f32[8,128]{1,0:T(8,128)}, f32[8,128]{1,0:T(8,128)}) custom-call(f32[3,8,64,256]{3,2,1,0:T(8,128)} %vel.1), custom_call_target="tpu_custom_call" | custom-call | tf_op jit(solution)/shard_map/germano/pallas_call | solution.py:421
  24.5 1.9 %scale.1 = (f32[1,64]{1,0:T(1,128)}, f32[8,64,256]{2,1,0:T(8,128)}) custom-call(f32[8,64,256]{2,1,0:T(8,128)} %get-tuple-element.7.strength, f32[8,128]{1,0:T(8,128)} %get-tuple-element.8.cexp, f32[8,128]{1,0:T(8,128)} %get-tuple-element.9.crow), custom_call_target="tpu_custom_call" | custom-call | tf_op jit(solution)/shard_map/scale/pallas_call | solution.py:454

commit v2 on v1

--- a/solution.py
+++ b/solution.py
@@ -16,136 +16,144 @@
 CHUNKS = 4
 CHUNK = YL // CHUNKS
 clip_high = 0.1
-
-
-def next_odd(a):
-    return pltpu.roll(a, HALF - 1, 1)
-
-
-def prev_even(a):
-    return pltpu.roll(a, 1, 1)
-
-
-def span_diff(even, odd):
-    return odd - prev_even(odd), next_odd(even) - even
-
-
-def span_sum(even, odd):
-    pair_even = even + odd
-    pair_odd = odd + next_odd(even)
-    return pair_even + prev_even(pair_odd), pair_even + pair_odd
-
-
-def gradients(ref, row, start, lead):
-    stream = [[None] * 2 for _ in range(3)]
-    wall = [[None] * 2 for _ in range(3)]
-    span = [None] * 3
-    middle = [[None] * 2 for _ in range(3)]
-    sides = [[None] * 2 for _ in range(3)]
+TINY = 1.2e-38
+PAIRS = ((0, 0), (1, 1), (2, 2), (0, 1), (0, 2), (1, 2))
+
+
+def shifted(even, odd):
+    return pltpu.roll(odd, 1, 1), pltpu.roll(even, HALF - 1, 1)
+
+
+def span_sum(even, odd, before, after):
+    pair = even + odd
+    return pair + (before + even), pair + (after + odd)
+
+
+def at(k):
+    return slice(8 * k, 8 * k + 8)
+
+
+def span_unit(w, zu, dz, zp, xi, k, products):
+    r = 6 + 8 * k
+    even = [w[xi, c, 0, r : r + 8, :] for c in range(3)]
+    odd = [w[xi, c, 1, r : r + 8, :] for c in range(3)]
+    before, after = [None] * 3, [None] * 3
     for c in range(3):
-        for h in range(2):
-            above = ref[row + 1, c, h, start : start + 8, :]
-            below = ref[row - 1, c, h, start : start + 8, :]
-            stream[c][h] = above - below
-            sides[c][h] = above + below if lead else None
-            wall[c][h] = (
-                ref[row, c, h, start + 1 : start + 9, :] - ref[row, c, h, start - 1 : start + 7, :]
+        before[c], after[c] = shifted(even[c], odd[c])
+    for c in range(3):
+        both = span_sum(even[c], odd[c], before[c], after[c])
+        zu[xi, c, 0, at(k), :], zu[xi, c, 1, at(k), :] = both
+        if products:
+            dz[xi - 1, c, 0, at(k), :] = odd[c] - before[c]
+            dz[xi - 1, c, 1, at(k), :] = after[c] - even[c]
+    if products:
+        for p, (a, b) in enumerate(PAIRS):
+            both = span_sum(
+                even[a] * even[b], odd[a] * odd[b], before[a] * before[b], after[a] * after[b]
             )
-            middle[c][h] = ref[row, c, h, start : start + 8, :]
-        span[c] = span_diff(middle[c][0], middle[c][1])
-    return stream, wall, span, middle, sides
-
-
-def tensor(stream, wall, span, h):
-    d0, d1, d2 = stream[0][h], wall[1][h], span[2][h]
-    t01 = wall[0][h] + 0.25 * stream[1][h]
-    t02 = span[0][h] + 0.5 * stream[2][h]
-    t12 = span[1][h] + 2.0 * wall[2][h]
+            zp[xi - 1, p, 0, at(k), :], zp[xi - 1, p, 1, at(k), :] = both
+
+
+def tensor(stream, wall, span):
+    d0, d1, d2 = stream[0], wall[1], span[2]
+    t01 = wall[0] + 0.25 * stream[1]
+    t02 = span[0] + 0.5 * stream[2]
+    t12 = span[1] + 2.0 * wall[2]
     square = t01 * t01 + 0.25 * (0.5 * (d0 * d0) + t02 * t02 + t12 * t12)
     square = square + (2.0 * (d1 * d1) + 0.5 * (d2 * d2))
-    return (d0, d1, d2, t01, t02, t12), jnp.sqrt(square)
-
-
-def strain_unit(w, st, vf, sr, xi, k):
+    return (d0, d1, d2, t01, t02, t12), square * lax.rsqrt(jnp.maximum(square, TINY))
+
+
+def strain_unit(w, zu, dz, zs, vf, dv, sr, xi, k):
     r = 6 + 8 * k
-    stream, wall, span, middle, sides = gradients(w, xi + 1, r, True)
+    stress = [None] * 2
     for h in range(2):
-        parts, mag = tensor(stream, wall, span, h)
+        stream = [
+            w[xi + 2, c, h, r : r + 8, :] - w[xi, c, h, r : r + 8, :] for c in range(3)
+        ]
+        wall = [
+            w[xi + 1, c, h, r + 1 : r + 9, :] - w[xi + 1, c, h, r - 1 : r + 7, :]
+            for c in range(3)
+        ]
+        span = [dz[xi, c, h, at(k), :] for c in range(3)]
+        parts, mag = tensor(stream, wall, span)
         quarter, half = 0.25 * mag, 0.5 * mag
         factors = (quarter, mag, half, half, quarter, quarter)
-        for p in range(6):
-            st[xi, p, h, 8 * k : 8 * k + 8, :] = factors[p] * parts[p]
-        sr[xi, h, 8 * k : 8 * k + 8, :] = mag
+        stress[h] = [factors[p] * parts[p] for p in range(6)]
+        sr[xi, h, at(k), :] = mag
+    for p in range(6):
+        before, after = shifted(stress[0][p], stress[1][p])
+        both = span_sum(stress[0][p], stress[1][p], before, after)
+        zs[xi, p, 0, at(k), :], zs[xi, p, 1, at(k), :] = both
     for c in range(3):
-        smooth = [sides[c][h] + (middle[c][h] + middle[c][h]) for h in range(2)]
-        both = span_sum(smooth[0], smooth[1])
+        smooth = []
         for h in range(2):
-            vf[xi, c, h, 8 + 8 * k : 16 + 8 * k, :] = 0.25 * both[h]
-
-
-def sums_unit(w, st, vf, acc, xo, k):
-    r = 6 + 8 * k
-    j = 8 * k
-    stream, wall, span, middle, _ = gradients(vf, xo + 1, 8 + j, False)
-    model = [[None] * 6 for _ in range(2)]
-    leonard = [[None] * 6 for _ in range(2)]
-    for p in range(6):
-        line = []
-        for h in range(2):
-            mid = st[xo + 1, p, h, j : j + 8, :]
-            line.append(
-                st[xo, p, h, j : j + 8, :] + st[xo + 2, p, h, j : j + 8, :] + (mid + mid)
-            )
-        both = span_sum(line[0], line[1])
-        for h in range(2):
-            model[h][p] = both[h]
-    for h in range(2):
-        parts, mag = tensor(stream, wall, span, h)
-        twice, four = 2.0 * mag, 4.0 * mag
-        factors = (mag, four, twice, twice, mag, mag)
-        for p in range(6):
-            model[h][p] = model[h][p] - factors[p] * parts[p]
-    rows = [
-        [[w[xo + 1 + i, c, h, r : r + 8, :] for h in range(2)] for c in range(3)] for i in range(3)
-    ]
-    for p, (a, b) in enumerate(((0, 0), (1, 1), (2, 2), (0, 1), (0, 2), (1, 2))):
-        line = []
-        for h in range(2):
-            mid = rows[1][a][h] * rows[1][b][h]
-            line.append(
-                rows[0][a][h] * rows[0][b][h] + rows[2][a][h] * rows[2][b][h] + (mid + mid)
-            )
-        both = span_sum(line[0], line[1])
-        for h in range(2):
-            leonard[h][p] = both[h] - middle[a][h] * middle[b][h]
+            mid = zu[xi + 1, c, h, at(k), :]
+            line = (zu[xi, c, h, at(k), :] + mid) + (zu[xi + 2, c, h, at(k), :] + mid)
+            smooth.append(0.25 * line)
+            vf[xi, c, h, 8 + 8 * k : 16 + 8 * k, :] = smooth[h]
+        before, after = shifted(smooth[0], smooth[1])
+        dv[xi, c, 0, at(k), :] = smooth[1] - before
+        dv[xi, c, 1, at(k), :] = after - smooth[0]
+
+
+def sums_unit(zs, zp, vf, dv, acc, xo, k):
+    j = 8 + 8 * k
     num = den = None
     for h in range(2):
-        lo, mo = leonard[h], model[h]
-        third = (lo[0] + lo[1] + lo[2]) * (1.0 / 3.0)
-        n_diag = (lo[0] - third) * mo[0] + (lo[1] - third) * mo[1] + (lo[2] - third) * mo[2]
-        n_off = lo[3] * mo[3] + lo[4] * mo[4] + lo[5] * mo[5]
-        d_diag = mo[0] * mo[0] + mo[1] * mo[1] + mo[2] * mo[2]
-        d_off = mo[3] * mo[3] + mo[4] * mo[4] + mo[5] * mo[5]
-        n = n_diag + (n_off + n_off)
-        d = d_diag + (d_off + d_off)
-        num = n if num is None else num + n
-        den = d if den is None else den + d
-    acc[0, j : j + 8, :] += num
-    acc[1, j : j + 8, :] += den
-
-
-def over_rows(base, count, body):
+
+        def lines(ref, p):
+            rows = [ref[xo + i, p, h, at(k), :] for i in range(4)]
+            pair = [rows[i] + rows[i + 1] for i in range(3)]
+            return pair[0] + pair[1], pair[1] + pair[2]
+
+        stress = [lines(zs, p) for p in range(6)]
+        product = [lines(zp, p) for p in range(6)]
+        for i in range(2):
+            xi = xo + 1 + i
+            stream = [
+                vf[xi + 1, c, h, j : j + 8, :] - vf[xi - 1, c, h, j : j + 8, :] for c in range(3)
+            ]
+            wall = [
+                vf[xi, c, h, j + 1 : j + 9, :] - vf[xi, c, h, j - 1 : j + 7, :]
+                for c in range(3)
+            ]
+            span = [dv[xi, c, h, at(k), :] for c in range(3)]
+            middle = [vf[xi, c, h, j : j + 8, :] for c in range(3)]
+            parts, mag = tensor(stream, wall, span)
+            twice, four = 2.0 * mag, 4.0 * mag
+            factors = (mag, four, twice, twice, mag, mag)
+            mo = [stress[p][i] - factors[p] * parts[p] for p in range(6)]
+            lo = [product[p][i] - middle[a] * middle[b] for p, (a, b) in enumerate(PAIRS)]
+            third = (lo[0] + lo[1] + lo[2]) * (1.0 / 3.0)
+            n_diag = (lo[0] - third) * mo[0] + (lo[1] - third) * mo[1] + (lo[2] - third) * mo[2]
+            n_off = lo[3] * mo[3] + lo[4] * mo[4] + lo[5] * mo[5]
+            d_diag = mo[0] * mo[0] + mo[1] * mo[1] + mo[2] * mo[2]
+            d_off = mo[3] * mo[3] + mo[4] * mo[4] + mo[5] * mo[5]
+            n = n_diag + (n_off + n_off)
+            d = d_diag + (d_off + d_off)
+            num = n if num is None else num + n
+            den = d if den is None else den + d
+    acc[0, at(k), :] += num
+    acc[1, at(k), :] += den
+
+
+def over_rows(base, count, body, each=1):
     def step(i, carry):
-        body(base + i)
+        for e in range(each):
+            body(base + each * i + e)
         return carry
 
-    lax.fori_loop(0, count, step, 0)
+    if count == each:
+        step(0, 0)
+    else:
+        lax.fori_loop(0, count // each, step, 0)
 
 
 def main_kernel(
     nx, ny,
-    vel, strength, cexp, crow,
-    nat, w, st, vf, sr, acc, msg, gath,
+    vel, coefficient, viscosity,
+    nat, w, zu, dz, zp, zs, vf, dv, sr, strength, acc, msg, gath,
     in_sem, slow_send, slow_recv, fast_send, fast_recv, wall_send, wall_recv,
     corner_send, corner_recv, sum_send, sum_recv,
 ):
@@ -251,26 +259,27 @@
     for c in range(1, CHUNKS):
         slow_copies[c].start()
 
+    def spans(ks, products=True):
+        return lambda xi: [span_unit(w, zu, dz, zp, xi, k, products) for k in ks]
+
     def strains(ks):
-        def body(xi):
-            for k in ks:
-                strain_unit(w, st, vf, sr, xi, k)
-
-        return body
+        return lambda xi: [strain_unit(w, zu, dz, zs, vf, dv, sr, xi, k) for k in ks]
 
     def sums(ks):
-        def body(xo):
-            for k in ks:
-                sums_unit(w, st, vf, acc, xo, k)
-
-        return body
-
+        return lambda i: [sums_unit(zs, zp, vf, dv, acc, 2 * i, k) for k in ks]
+
+    inner = range(1, 8)
     fast_first = 8 - 8 * core
-    near_first = 2 - 2 * core
-    over_rows(2, 6, strains(range(1, 8)))
+    near_pair = 1 - core
+    fast_inner, fast_outer = 10 - 9 * core, 11 - 11 * core
+    slow_inner, slow_outer = 1 + 9 * core, 11 * core
+    over_rows(2, 8, spans(inner))
+    over_rows(2, 6, strains(inner))
     fast_copy.wait_recv()
-    over_rows(fast_first, 2, strains(range(1, 8)))
-    over_rows(near_first, 6, sums(range(2, 7)))
+    spans(inner)(fast_inner)
+    spans(inner, False)(fast_outer)
+    over_rows(fast_first, 2, strains(inner))
+    over_rows(near_pair, 3, sums(range(2, 7)))
 
     corner_slow_low = edge(
         (slow_src, 2), (slow_dst, 2), 6, 6, 2, (corner_send.at[0], corner_recv.at[0]), (slow, my)
@@ -297,14 +306,17 @@
         corner_slow_high.start()
         corner_fast_high.start()
 
-    over_rows(2, 6, strains((0, 8)))
+    over_rows(2, 8, spans((0, 8)), 4)
+    over_rows(2, 6, strains((0, 8)), 3)
     pl.when(has_low)(corner_fast_low.wait_recv)
     pl.when(has_high)(corner_fast_high.wait_recv)
-    over_rows(fast_first, 2, strains((0, 8)))
-    over_rows(near_first, 6, sums((0, 1, 7, 8)))
+    spans((0, 8))(fast_inner)
+    spans((0, 8), False)(fast_outer)
+    over_rows(fast_first, 2, strains((0, 8)), 2)
+    over_rows(near_pair, 3, sums((0, 1, 7, 8)))
 
     slow_first = 8 * core
-    far_first = 6 * core
+    far_pair = 3 * core
     groups = (((0, 1), (0,)), ((2, 3), (1, 2)), ((4, 5), (3, 4)), ((6, 7, 8), (5, 6, 7, 8)))
     for c in range(CHUNKS):
         slow_copies[c].wait_recv()
@@ -312,8 +324,10 @@
             pl.when(has_low)(corner_slow_low.wait_recv)
         if c == CHUNKS - 1:
             pl.when(has_high)(corner_slow_high.wait_recv)
-        over_rows(slow_first, 2, strains(groups[c][0]))
-        over_rows(far_first, 2, sums(groups[c][1]))
+        spans(groups[c][0])(slow_inner)
+        spans(groups[c][0], False)(slow_outer)
+        over_rows(slow_first, 2, strains(groups[c][0]), 2)
+        sums(groups[c][1])(far_pair)
 
     packs = []
     for q in range(2):
@@ -378,13 +392,23 @@
     above = jnp.where(jnp.logical_and(lane == 24, jnp.logical_not(has_high)), raw, above)
     smooth = 0.25 * below + 0.5 * raw + 0.25 * above
     row = lane + 2
-    crow[...] = jnp.take_along_axis(
+    line = jnp.take_along_axis(
         smooth, lax.rem(16 * lax.rem(row, 8) + lax.div(row, 8), HALF), axis=1
     )
+    coefficient[...] = line[0:1, 0:YL]
     row = 8 * lane + sub + 2
-    cexp[...] = jnp.take_along_axis(
+    table = jnp.take_along_axis(
         smooth, lax.rem(16 * lax.rem(row, 8) + lax.div(row, 8), HALF), axis=1
     )
+    columns = [jnp.broadcast_to(table[:, m : m + 1], (8, HALF)) for m in range(8)]
+
+    def scale(x):
+        for m in range(8):
+            for side in range(2):
+                part = (x, at(m), slice(HALF * side, HALF * side + HALF))
+                viscosity[part] = strength[part] * columns[m]
+
+    over_rows(0, XL, scale, 2)
 
     for copy in slow_copies:
         copy.wait_send()
@@ -405,34 +429,28 @@
     everyone.wait_send()
 
 
-def scale_kernel(strength, cexp, crow, coefficient, viscosity):
-    coefficient[...] = crow[0:1, 0:YL]
-    for m in range(8):
-        column = cexp[:, m : m + 1]
-        for x in range(XL):
-            for side in range(2):
-                at = (x, slice(8 * m, 8 * m + 8), slice(128 * side, 128 * side + 128))
-                viscosity[at] = strength[at] * column
-
-
 def local(nx, ny, velocity):
     vmem = pl.BlockSpec(memory_space=pltpu.VMEM)
     dma = pltpu.SemaphoreType.DMA
-    strength, cexp, crow = pl.pallas_call(
+    coefficient, viscosity = pl.pallas_call(
         functools.partial(main_kernel, nx, ny),
         out_shape=(
-            jax.ShapeDtypeStruct((XL, YL, ZL), F32),
-            jax.ShapeDtypeStruct((8, HALF), F32),
-            jax.ShapeDtypeStruct((8, HALF), F32),
+            pltpu.VMEM((1, YL), F32),
+            pltpu.VMEM((XL, YL, ZL), F32),
         ),
         in_specs=[pl.BlockSpec(memory_space=pl.ANY)],
-        out_specs=(vmem, vmem, vmem),
+        out_specs=(vmem, vmem),
         scratch_shapes=[
             pltpu.VMEM((3, XL, YL, ZL), F32),
             pltpu.VMEM((12, 3, 2, 80, HALF), F32),
+            pltpu.VMEM((12, 3, 2, 72, HALF), F32),
+            pltpu.VMEM((10, 3, 2, 72, HALF), F32),
+            pltpu.VMEM((10, 6, 2, 72, HALF), F32),
             pltpu.VMEM((10, 6, 2, 72, HALF), F32),
             pltpu.VMEM((10, 3, 2, 88, HALF), F32),
+            pltpu.VMEM((10, 3, 2, 72, HALF), F32),
             pltpu.VMEM((10, 2, 72, HALF), F32),
+            pltpu.VMEM((XL, YL, ZL), F32),
             pltpu.VMEM((2, 72, HALF), F32),
             pltpu.VMEM((2, HALF), F32),
             pltpu.VMEM((nx, 2, HALF), F32),
@@ -451,16 +469,6 @@
         compiler_params=pltpu.CompilerParams(collective_id=0, has_side_effects=True),
         name="germano",
     )(velocity)
-    coefficient, viscosity = pl.pallas_call(
-        scale_kernel,
-        out_shape=(
-            jax.ShapeDtypeStruct((1, YL), F32),
-            jax.ShapeDtypeStruct((XL, YL, ZL), F32),
-        ),
-        in_specs=[vmem, vmem, vmem],
-        out_specs=(vmem, vmem),
-        name="scale",
-    )(strength, cexp, crow)
     return coefficient.reshape(YL), viscosity
 
 

time: 26.6 us -> 23.4 us (0.88)
  Pallas kernels: 25.8 us -> 21.1 us
  local copies, waits for them, and re-layouts: 0 us -> 1.31 us
    pallas_call x2 -> x1, Pallas kernels: 25.8 us -> 21.1 us  [local(): pl.pallas_call(functools.partial(main_kernel, nx, ny), out_shape=(pltpu.V...]
    unnamed x0 -> x2, local copies, waits for them, and re-layouts: none -> 1.31 us
where the time goes in v2:
time: 23.4 us; the launch traced here: 23 us
  Pallas kernels  21.1 us (90%)
  local copies, waits for them, and re-layouts  1.31 us (6%)
  between operations  0.64 us (3%)
    pallas_call x1, Pallas kernels, local(): pl.pallas_call(functools.partial(main_kernel, nx, ny), out_shape=(pltpu.V...  21.1 us
    unnamed x2, local copies, waits for them, and re-layouts  1.31 us

profile of v2, /device:TPU:1, one launch (start us, length us, event | category | flops | bytes accessed | tf_op | source)
XLA Modules:
  0.0 23.0 jit_solution(16867603382586391638)
XLA Ops:
  0.6 21.1 %germano.1 = (f32[1,64]{1,0:T(1,128)S(1)}, f32[8,64,256]{2,1,0:T(8,128)S(1)}) custom-call(f32[3,8,64,256]{3,2,1,0:T(8,128)} %vel.1), custom_call_target="tpu_custom_call" | custom-call | tf_op jit(solution)/shard_map/germano/pallas_call | solution.py:435
  21.7 0.5 %copy.5 = f32[64]{0:T(128)} copy(f32[64]{0:T(128)S(1)} %bitcast.1) | data formatting | bytes 512
  22.2 0.8 %copy.6 = f32[8,64,256]{2,1,0:T(8,128)} copy(f32[8,64,256]{2,1,0:T(8,128)S(1)} %get-tuple-element.7) | data formatting | bytes 1048576

commit v3 on v2

--- a/solution.py
+++ b/solution.py
@@ -8,13 +8,14 @@
 from jax.sharding import PartitionSpec as P
 
 F32 = jnp.float32
+BF16 = jnp.bfloat16
 MESH = pl.DeviceIdType.MESH
 XL = 8
 YL = 64
 ZL = 256
 HALF = 128
-CHUNKS = 4
-CHUNK = YL // CHUNKS
+CUTS = (0, 24, 48, 56, 64)
+CHUNKS = len(CUTS) - 1
 clip_high = 0.1
 TINY = 1.2e-38
 PAIRS = ((0, 0), (1, 1), (2, 2), (0, 1), (0, 2), (1, 2))
@@ -153,7 +154,7 @@
 def main_kernel(
     nx, ny,
     vel, coefficient, viscosity,
-    nat, w, zu, dz, zp, zs, vf, dv, sr, strength, acc, msg, gath,
+    nat, w, zu, dz, zp, zs, vf, dv, sr, strength, acc, msg, gath, order,
     in_sem, slow_send, slow_recv, fast_send, fast_recv, wall_send, wall_recv,
     corner_send, corner_recv, sum_send, sum_recv,
 ):
@@ -167,28 +168,23 @@
     has_low = my > 0
     has_high = my < ny - 1
 
+    def base(q):
+        return core * q + (1 - core) * (10 - q)
+
+    def signal(sem, x, y):
+        pl.semaphore_signal(sem, inc=1, device_id=(x, y), device_id_type=MESH)
+
+    loads = []
+    for g, q in enumerate((8, 6, 4, 2)):
+        cells = pl.ds(base(q) - 2, 2)
+        loads.append(pltpu.make_async_copy(vel.at[:, cells], nat.at[:, cells], in_sem.at[g]))
+        loads[g].start()
+
     barrier = pltpu.get_barrier_semaphore()
     for p in range(1, nx):
-        pl.semaphore_signal(
-            barrier, inc=1, device_id=(lax.rem(mx + p, nx), my), device_id_type=MESH
-        )
-
-    @pl.when(has_low)
-    def _():
-        pl.semaphore_signal(barrier, inc=1, device_id=(mx, my - 1), device_id_type=MESH)
-
-    @pl.when(has_high)
-    def _():
-        pl.semaphore_signal(barrier, inc=1, device_id=(mx, my + 1), device_id_type=MESH)
-
-    loads = [
-        pltpu.make_async_copy(
-            vel.at[:, 2 * g : 2 * g + 2], nat.at[:, 2 * g : 2 * g + 2], in_sem.at[g]
-        )
-        for g in range(4)
-    ]
-    for load in loads:
-        load.start()
+        signal(barrier, lax.rem(mx + p, nx), my)
+    pl.when(has_low)(lambda: signal(barrier, mx, my - 1))
+    pl.when(has_high)(lambda: signal(barrier, mx, my + 1))
 
     def clear(first, count):
         def body(x):
@@ -206,29 +202,26 @@
 
     lane = lax.broadcasted_iota(jnp.int32, (8, HALF), 1)
     sub = lax.broadcasted_iota(jnp.int32, (8, HALF), 0)
-    low_lane = lane < 64
-    pick_left = lax.rem(lane, 64) * 2 + lax.div(lane, 64)
-    pick_right = lax.rem(lane, 64) * 2 + (1 - lax.div(lane, 64))
-
-    def split(x):
+    source = lax.broadcasted_iota(jnp.int32, (ZL, ZL), 0)
+    target = lax.broadcasted_iota(jnp.int32, (ZL, ZL), 1)
+    wanted = 2 * lax.rem(target, HALF) + lax.div(target, HALF)
+    order[...] = jnp.where(source == wanted, 1.0, 0.0).astype(BF16)
+
+    def split(row):
+        cells = jnp.concatenate([nat[c, row - 2] for c in range(3)], axis=0)
+        high = cells.astype(BF16)
+        rest = cells - high.astype(F32)
+        mid = rest.astype(BF16)
+        low = (rest - mid.astype(F32)).astype(BF16)
+        high, mid, low = (
+            jnp.dot(part, order[...], preferred_element_type=F32) for part in (high, mid, low)
+        )
+        cells = high + (mid + low)
         for c in range(3):
-            for m in range(8):
-                a = nat[c, x, 8 * m : 8 * m + 8, 0:128]
-                b = nat[c, x, 8 * m : 8 * m + 8, 128:256]
-                a = jnp.take_along_axis(a, pick_left, axis=1)
-                b = jnp.take_along_axis(b, pick_right, axis=1)
-                w[x + 2, c, 0, 8 + 8 * m : 16 + 8 * m, :] = jnp.where(low_lane, a, b)
-                w[x + 2, c, 1, 8 + 8 * m : 16 + 8 * m, :] = pltpu.roll(
-                    jnp.where(low_lane, b, a), 64, 1
-                )
-
-    for g in range(4):
-        loads[g].wait()
-        over_rows(2 * g, 2, split)
-
-    pl.semaphore_wait(
-        barrier, nx - 1 + has_low.astype(jnp.int32) + has_high.astype(jnp.int32)
-    )
+            for h in range(2):
+                w[row, c, h, 8 : 8 + YL, :] = cells[
+                    YL * c : YL * c + YL, HALF * h : HALF * h + HALF
+                ]
 
     def edge(src, dst, rows_from, rows_to, count, sems, to):
         return pltpu.make_async_remote_copy(
@@ -244,115 +237,134 @@
     fast_src, fast_dst = 8 - 6 * core, 10 * core
     slow_copies = [
         edge(
-            (slow_src, 2), (slow_dst, 2), 8 + CHUNK * c, 8 + CHUNK * c, CHUNK,
+            (slow_src, 2), (slow_dst, 2), 8 + lo, 8 + lo, hi - lo,
             (slow_send.at[c], slow_recv.at[c]), (slow, my),
         )
-        for c in range(CHUNKS)
+        for c, (lo, hi) in enumerate(zip(CUTS[:-1], CUTS[1:]))
     ]
     fast_copy = edge((fast_src, 2), (fast_dst, 2), 8, 8, YL, (fast_send, fast_recv), (fast, my))
     to_low = edge((2, 8), (2, 8), 8, 72, 2, (wall_send.at[0], wall_recv.at[0]), (mx, my - 1))
     to_high = edge((2, 8), (2, 8), 70, 6, 2, (wall_send.at[1], wall_recv.at[1]), (mx, my + 1))
+    corners = [
+        edge(rows[0], rows[1], r, r, 2, (corner_send.at[i], corner_recv.at[i]), (to, my))
+        for i, (rows, to, r) in enumerate(
+            (
+                (((slow_src, 2), (slow_dst, 2)), slow, 6),
+                (((slow_src, 2), (slow_dst, 2)), slow, 72),
+                (((fast_src, 2), (fast_dst, 2)), fast, 6),
+                (((fast_src, 2), (fast_dst, 2)), fast, 72),
+            )
+        )
+    ]
+
+    def spans(q, ks, products=(True, True)):
+        for e in range(2):
+            for k in ks:
+                if products[0] == products[1]:
+                    span_unit(w, zu, dz, zp, base(q) + e, k, products[0])
+                else:
+                    row = base(q) + (core if e else 1 - core)
+                    span_unit(w, zu, dz, zp, row, k, products[e])
+
+    def strains(q, ks):
+        for e in range(2):
+            for k in ks:
+                strain_unit(w, zu, dz, zs, vf, dv, sr, base(q) - 1 + e, k)
+
+    def sums(q, ks):
+        for k in ks:
+            sums_unit(zs, zp, vf, dv, acc, base(q) - 2, k)
+
+    inner = range(1, 8)
+    loads[0].wait()
+    split(base(8))
+    split(base(8) + 1)
+    for g, q in ((1, 6), (2, 4), (3, 2)):
+        loads[g].wait()
+        spans(q + 2, inner)
+        split(base(q))
+        split(base(q) + 1)
+    strains(7, inner)
+    spans(2, inner)
+    pl.semaphore_wait(
+        barrier, nx - 1 + has_low.astype(jnp.int32) + has_high.astype(jnp.int32)
+    )
     slow_copies[0].start()
     pl.when(has_low)(to_low.start)
     pl.when(has_high)(to_high.start)
     fast_copy.start()
-    for c in range(1, CHUNKS):
-        slow_copies[c].start()
-
-    def spans(ks, products=True):
-        return lambda xi: [span_unit(w, zu, dz, zp, xi, k, products) for k in ks]
-
-    def strains(ks):
-        return lambda xi: [strain_unit(w, zu, dz, zs, vf, dv, sr, xi, k) for k in ks]
-
-    def sums(ks):
-        return lambda i: [sums_unit(zs, zp, vf, dv, acc, 2 * i, k) for k in ks]
-
-    inner = range(1, 8)
-    fast_first = 8 - 8 * core
-    near_pair = 1 - core
-    fast_inner, fast_outer = 10 - 9 * core, 11 - 11 * core
-    slow_inner, slow_outer = 1 + 9 * core, 11 * core
-    over_rows(2, 8, spans(inner))
-    over_rows(2, 6, strains(inner))
+    for copy in slow_copies[1:]:
+        copy.start()
+
+    strains(5, inner)
+    sums(6, range(2, 7))
+    strains(3, inner)
     fast_copy.wait_recv()
-    spans(inner)(fast_inner)
-    spans(inner, False)(fast_outer)
-    over_rows(fast_first, 2, strains(inner))
-    over_rows(near_pair, 3, sums(range(2, 7)))
-
-    corner_slow_low = edge(
-        (slow_src, 2), (slow_dst, 2), 6, 6, 2, (corner_send.at[0], corner_recv.at[0]), (slow, my)
-    )
-    corner_slow_high = edge(
-        (slow_src, 2), (slow_dst, 2), 72, 72, 2, (corner_send.at[1], corner_recv.at[1]), (slow, my)
-    )
-    corner_fast_low = edge(
-        (fast_src, 2), (fast_dst, 2), 6, 6, 2, (corner_send.at[2], corner_recv.at[2]), (fast, my)
-    )
-    corner_fast_high = edge(
-        (fast_src, 2), (fast_dst, 2), 72, 72, 2, (corner_send.at[3], corner_recv.at[3]), (fast, my)
-    )
+    sums(4, range(2, 7))
+    spans(0, inner, (False, True))
+    strains(1, inner)
+    sums(2, range(2, 7))
 
     @pl.when(has_low)
     def _():
         to_high.wait_recv()
-        corner_slow_low.start()
-        corner_fast_low.start()
+        corners[0].start()
+        corners[2].start()
 
     @pl.when(has_high)
     def _():
         to_low.wait_recv()
-        corner_slow_high.start()
-        corner_fast_high.start()
-
-    over_rows(2, 8, spans((0, 8)), 4)
-    over_rows(2, 6, strains((0, 8)), 3)
-    pl.when(has_low)(corner_fast_low.wait_recv)
-    pl.when(has_high)(corner_fast_high.wait_recv)
-    spans((0, 8))(fast_inner)
-    spans((0, 8), False)(fast_outer)
-    over_rows(fast_first, 2, strains((0, 8)), 2)
-    over_rows(near_pair, 3, sums((0, 1, 7, 8)))
-
-    slow_first = 8 * core
-    far_pair = 3 * core
-    groups = (((0, 1), (0,)), ((2, 3), (1, 2)), ((4, 5), (3, 4)), ((6, 7, 8), (5, 6, 7, 8)))
-    for c in range(CHUNKS):
-        slow_copies[c].wait_recv()
+        corners[1].start()
+        corners[3].start()
+
+    for q in (8, 6, 4, 2):
+        spans(q, (0, 8))
+    for q in (7, 5, 3):
+        strains(q, (0, 8))
+    pl.when(has_low)(corners[2].wait_recv)
+    pl.when(has_high)(corners[3].wait_recv)
+    sums(6, (0, 1, 7, 8))
+    spans(0, (0, 8), (False, True))
+    sums(4, (0, 1, 7, 8))
+    strains(1, (0, 8))
+    sums(2, (0, 1, 7, 8))
+
+    done_strains = done_sums = 0
+    for c, copy in enumerate(slow_copies):
+        last = c == len(slow_copies) - 1
+        copy.wait_recv()
         if c == 0:
-            pl.when(has_low)(corner_slow_low.wait_recv)
-        if c == CHUNKS - 1:
-            pl.when(has_high)(corner_slow_high.wait_recv)
-        spans(groups[c][0])(slow_inner)
-        spans(groups[c][0], False)(slow_outer)
-        over_rows(slow_first, 2, strains(groups[c][0]), 2)
-        sums(groups[c][1])(far_pair)
+            pl.when(has_low)(corners[0].wait_recv)
+        if last:
+            pl.when(has_high)(corners[1].wait_recv)
+        ready_strains = 9 if last else (CUTS[c + 1] + 1) // 8
+        ready_sums = 9 if last else ready_strains - 1
+        spans(10, range(done_strains, ready_strains), (True, False))
+        strains(9, range(done_strains, ready_strains))
+        sums(8, range(done_sums, ready_sums))
+        done_strains, done_sums = ready_strains, ready_sums
 
     packs = []
-    for q in range(2):
+    for p in range(2):
         table = jnp.zeros((8, HALF), F32)
         for k in range(9):
-            column = jnp.sum(acc[q, 8 * k : 8 * k + 8, :], axis=1, keepdims=True)
+            column = jnp.sum(acc[p, at(k), :], axis=1, keepdims=True)
             table = jnp.where(lane == k, column, table)
         spread = pltpu.roll(table, 0, 1, stride=16, stride_axis=0)
         packs.append(jnp.sum(spread, axis=0, keepdims=True))
-    for q in range(2):
-        msg[q : q + 1, :] = packs[q]
-        gath[mx, q : q + 1, :] = packs[q]
-
-    def gather_copy(to):
-        return pltpu.make_async_remote_copy(
+    for p in range(2):
+        msg[p : p + 1, :] = packs[p]
+        gath[mx, p : p + 1, :] = packs[p]
+
+    for p in range(1, nx):
+        pltpu.make_async_remote_copy(
             src_ref=msg,
             dst_ref=gath.at[mx],
             send_sem=sum_send,
             recv_sem=sum_recv,
-            device_id=(to, my),
+            device_id=(lax.rem(mx + p, nx), my),
             device_id_type=MESH,
-        )
-
-    for p in range(1, nx):
-        gather_copy(lax.rem(mx + p, nx)).start()
+        ).start()
 
     even_lane = lax.rem(lane, 2) == 0
     pick_low = lax.div(lane, 2)
@@ -362,14 +374,14 @@
         for m in range(8):
             even = sr[x + 1, 0, 8 * m + 2 : 8 * m + 10, :]
             odd = sr[x + 1, 1, 8 * m + 2 : 8 * m + 10, :]
-            for side, pick in enumerate((pick_low, pick_high)):
-                strength[x, 8 * m : 8 * m + 8, 128 * side : 128 * side + 128] = jnp.where(
+            for side, source in enumerate((pick_low, pick_high)):
+                strength[x, at(m), HALF * side : HALF * side + HALF] = jnp.where(
                     even_lane,
-                    jnp.take_along_axis(even, pick, axis=1),
-                    jnp.take_along_axis(odd, pick, axis=1),
+                    jnp.take_along_axis(even, source, axis=1),
+                    jnp.take_along_axis(odd, source, axis=1),
                 )
 
-    over_rows(0, XL, join)
+    over_rows(0, XL, join, 2)
 
     everyone = pltpu.make_async_remote_copy(
         src_ref=gath.at[0 : nx - 1],
@@ -417,16 +429,27 @@
     @pl.when(has_low)
     def _():
         to_low.wait_send()
-        corner_slow_low.wait_send()
-        corner_fast_low.wait_send()
+        corners[0].wait_send()
+        corners[2].wait_send()
 
     @pl.when(has_high)
     def _():
         to_high.wait_send()
-        corner_slow_high.wait_send()
-        corner_fast_high.wait_send()
+        corners[1].wait_send()
+        corners[3].wait_send()
 
     everyone.wait_send()
+
+
+def store_kernel(coefficient, viscosity, coefficient_out, viscosity_out, sems):
+    copies = [
+        pltpu.make_async_copy(viscosity, viscosity_out, sems.at[0]),
+        pltpu.make_async_copy(coefficient, coefficient_out, sems.at[1]),
+    ]
+    for copy in copies:
+        copy.start()
+    for copy in copies:
+        copy.wait()
 
 
 def local(nx, ny, velocity):
@@ -454,6 +477,7 @@
             pltpu.VMEM((2, 72, HALF), F32),
             pltpu.VMEM((2, HALF), F32),
             pltpu.VMEM((nx, 2, HALF), F32),
+            pltpu.VMEM((ZL, ZL), BF16),
             dma((4,)),
             dma((CHUNKS,)),
             dma((CHUNKS,)),
@@ -469,6 +493,21 @@
         compiler_params=pltpu.CompilerParams(collective_id=0, has_side_effects=True),
         name="germano",
     )(velocity)
+    anywhere = pl.BlockSpec(memory_space=pl.ANY)
+    coefficient, viscosity = pl.pallas_call(
+        store_kernel,
+        out_shape=(
+            jax.ShapeDtypeStruct((1, YL), F32),
+            jax.ShapeDtypeStruct((XL, YL, ZL), F32),
+        ),
+        in_specs=[vmem, vmem],
+        out_specs=(anywhere, anywhere),
+        scratch_shapes=[dma((2,))],
+        name="store",
+    )(
+        pltpu.with_memory_space_constraint(coefficient, pltpu.VMEM),
+        pltpu.with_memory_space_constraint(viscosity, pltpu.VMEM),
+    )
     return coefficient.reshape(YL), viscosity
 
 

time: 23.4 us -> 22.7 us (0.970)
  the two profiles are of different devices: /device:TPU:1 before, /device:TPU:9 now
where the time goes in v3:
time: 22.7 us; the launch traced here: 22.6 us
  Pallas kernels  21.9 us (96%)
  between operations  0.64 us (3%)
    pallas_call x1, Pallas kernels, local(): pl.pallas_call(functools.partial(main_kernel, nx, ny), out_shape=(pltpu.V...  21.1 us
    pallas_call x1, Pallas kernels, local(): pl.pallas_call(store_kernel, out_shape=(jax.ShapeDtypeStruct((1, YL), F32...  0.81 us

profile of v3, /device:TPU:9, one launch (start us, length us, event | category | flops | bytes accessed | tf_op | source)
XLA Modules:
  0.0 22.6 jit_solution(2466792418427665160)
XLA Ops:
  0.6 21.1 %germano.1 = (f32[1,64]{1,0:T(1,128)S(1)}, f32[8,64,256]{2,1,0:T(8,128)S(1)}) custom-call(f32[3,8,64,256]{3,2,1,0:T(8,128)} %vel.1), custom_call_target="tpu_custom_call" | custom-call | tf_op jit(solution)/shard_map/germano/pallas_call | solution.py:458
  21.8 0.8 %store.1 = (f32[1,64]{1,0:T(1,128)}, f32[8,64,256]{2,1,0:T(8,128)}) custom-call(f32[1,64]{1,0:T(1,128)S(1)} %get-tuple-element.6.coefficient, f32[8,64,256]{2,1,0:T(8,128)S(1)} %get-tuple-element.7.viscosity), custom_call_target="tpu_custom_call" | custom-call | tf_op jit(solution)/shard_map/store/pallas_call | solution.py:497

commit v4 on v3

--- a/solution.py
+++ b/solution.py
@@ -65,7 +65,7 @@
     return (d0, d1, d2, t01, t02, t12), square * lax.rsqrt(jnp.maximum(square, TINY))
 
 
-def strain_unit(w, zu, dz, zs, vf, dv, sr, xi, k):
+def strain_unit(w, zu, dz, zs, vf, sr, xi, k):
     r = 6 + 8 * k
     stress = [None] * 2
     for h in range(2):
@@ -87,20 +87,24 @@
         both = span_sum(stress[0][p], stress[1][p], before, after)
         zs[xi, p, 0, at(k), :], zs[xi, p, 1, at(k), :] = both
     for c in range(3):
-        smooth = []
         for h in range(2):
             mid = zu[xi + 1, c, h, at(k), :]
             line = (zu[xi, c, h, at(k), :] + mid) + (zu[xi + 2, c, h, at(k), :] + mid)
-            smooth.append(0.25 * line)
-            vf[xi, c, h, 8 + 8 * k : 16 + 8 * k, :] = smooth[h]
-        before, after = shifted(smooth[0], smooth[1])
-        dv[xi, c, 0, at(k), :] = smooth[1] - before
-        dv[xi, c, 1, at(k), :] = after - smooth[0]
-
-
-def sums_unit(zs, zp, vf, dv, acc, xo, k):
+            vf[xi, c, h, 8 + 8 * k : 16 + 8 * k, :] = 0.25 * line
+
+
+def sums_unit(zs, zp, vf, acc, xo, k):
     j = 8 + 8 * k
     num = den = None
+    middles, spans = [], []
+    for i in range(2):
+        middle = [[vf[xo + 1 + i, c, h, j : j + 8, :] for h in range(2)] for c in range(3)]
+        span = []
+        for even, odd in middle:
+            before, after = shifted(even, odd)
+            span.append((odd - before, after - even))
+        middles.append(middle)
+        spans.append(span)
     for h in range(2):
 
         def lines(ref, p):
@@ -119,8 +123,8 @@
                 vf[xi, c, h, j + 1 : j + 9, :] - vf[xi, c, h, j - 1 : j + 7, :]
                 for c in range(3)
             ]
-            span = [dv[xi, c, h, at(k), :] for c in range(3)]
-            middle = [vf[xi, c, h, j : j + 8, :] for c in range(3)]
+            span = [spans[i][c][h] for c in range(3)]
+            middle = [middles[i][c][h] for c in range(3)]
             parts, mag = tensor(stream, wall, span)
             twice, four = 2.0 * mag, 4.0 * mag
             factors = (mag, four, twice, twice, mag, mag)
@@ -154,7 +158,7 @@
 def main_kernel(
     nx, ny,
     vel, coefficient, viscosity,
-    nat, w, zu, dz, zp, zs, vf, dv, sr, strength, acc, msg, gath, order,
+    nat, w, zu, dz, zp, zs, vf, sr, strength, acc, msg, gath, order,
     in_sem, slow_send, slow_recv, fast_send, fast_recv, wall_send, wall_recv,
     corner_send, corner_recv, sum_send, sum_recv,
 ):
@@ -171,20 +175,32 @@
     def base(q):
         return core * q + (1 - core) * (10 - q)
 
+    def peers(far_first):
+        if nx != 32:
+            return [lax.rem(mx + p, nx) for p in range(1, nx)]
+        px, pz = mx // 8, lax.rem(mx, 8) // 2
+        xs = [lax.rem(px + d, 4) * 8 for d in range(4)]
+        zs_ = [lax.rem(pz + d, 4) * 2 for d in range(4)]
+        steps = [(a, b, c) for a in range(4) for b in range(4) for c in range(2)][1:]
+        steps.sort(key=lambda t: min(t[0], 4 - t[0]) + min(t[1], 4 - t[1]), reverse=far_first)
+        return [xs[a] + (zs_[b] + (1 - core if c else core)) for a, b, c in steps]
+
     def signal(sem, x, y):
         pl.semaphore_signal(sem, inc=1, device_id=(x, y), device_id_type=MESH)
 
+    barrier = pltpu.get_barrier_semaphore()
     loads = []
     for g, q in enumerate((8, 6, 4, 2)):
         cells = pl.ds(base(q) - 2, 2)
         loads.append(pltpu.make_async_copy(vel.at[:, cells], nat.at[:, cells], in_sem.at[g]))
-        loads[g].start()
-
-    barrier = pltpu.get_barrier_semaphore()
-    for p in range(1, nx):
-        signal(barrier, lax.rem(mx + p, nx), my)
+        if g == 0:
+            loads[g].start()
+    for peer in peers(True):
+        signal(barrier, peer, my)
     pl.when(has_low)(lambda: signal(barrier, mx, my - 1))
     pl.when(has_high)(lambda: signal(barrier, mx, my + 1))
+    for load in loads[1:]:
+        load.start()
 
     def clear(first, count):
         def body(x):
@@ -207,8 +223,9 @@
     wanted = 2 * lax.rem(target, HALF) + lax.div(target, HALF)
     order[...] = jnp.where(source == wanted, 1.0, 0.0).astype(BF16)
 
-    def split(row):
-        cells = jnp.concatenate([nat[c, row - 2] for c in range(3)], axis=0)
+    def split(row, lo=0, hi=YL):
+        rows = hi - lo
+        cells = jnp.concatenate([nat[c, row - 2, lo:hi, :] for c in range(3)], axis=0)
         high = cells.astype(BF16)
         rest = cells - high.astype(F32)
         mid = rest.astype(BF16)
@@ -219,8 +236,8 @@
         cells = high + (mid + low)
         for c in range(3):
             for h in range(2):
-                w[row, c, h, 8 : 8 + YL, :] = cells[
-                    YL * c : YL * c + YL, HALF * h : HALF * h + HALF
+                w[row, c, h, 8 + lo : 8 + hi, :] = cells[
+                    rows * c : rows * c + rows, HALF * h : HALF * h + HALF
                 ]
 
     def edge(src, dst, rows_from, rows_to, count, sems, to):
@@ -269,36 +286,60 @@
     def strains(q, ks):
         for e in range(2):
             for k in ks:
-                strain_unit(w, zu, dz, zs, vf, dv, sr, base(q) - 1 + e, k)
+                strain_unit(w, zu, dz, zs, vf, sr, base(q) - 1 + e, k)
 
     def sums(q, ks):
         for k in ks:
-            sums_unit(zs, zp, vf, dv, acc, base(q) - 2, k)
+            sums_unit(zs, zp, vf, acc, base(q) - 2, k)
 
     inner = range(1, 8)
+    px, pz = mx // 8, lax.rem(mx, 8) // 2
+    either, both = jnp.logical_or, jnp.logical_and
+    first = either(pz == 0, both(pz == 1, px < 2))
+    second = either(
+        both(pz == 1, px >= 2), either(both(pz == 2, px < 2), both(pz == 3, px == 0))
+    )
+    third = jnp.logical_not(either(first, second))
+
+    def meet():
+        pl.semaphore_wait(
+            barrier, nx - 1 + has_low.astype(jnp.int32) + has_high.astype(jnp.int32)
+        )
+        for copy in slow_copies:
+            copy.start()
+
+    def send_near():
+        pl.when(has_low)(to_low.start)
+        pl.when(has_high)(to_high.start)
+        fast_copy.start()
+
     loads[0].wait()
     split(base(8))
     split(base(8) + 1)
+    pl.when(third)(meet)
     for g, q in ((1, 6), (2, 4), (3, 2)):
         loads[g].wait()
         spans(q + 2, inner)
         split(base(q))
         split(base(q) + 1)
+    pl.when(third)(send_near)
     strains(7, inner)
     spans(2, inner)
-    pl.semaphore_wait(
-        barrier, nx - 1 + has_low.astype(jnp.int32) + has_high.astype(jnp.int32)
-    )
-    slow_copies[0].start()
-    pl.when(has_low)(to_low.start)
-    pl.when(has_high)(to_high.start)
-    fast_copy.start()
-    for copy in slow_copies[1:]:
-        copy.start()
+
+    @pl.when(second)
+    def _():
+        meet()
+        send_near()
 
     strains(5, inner)
     sums(6, range(2, 7))
     strains(3, inner)
+
+    @pl.when(first)
+    def _():
+        meet()
+        send_near()
+
     fast_copy.wait_recv()
     sums(4, range(2, 7))
     spans(0, inner, (False, True))
@@ -356,13 +397,13 @@
         msg[p : p + 1, :] = packs[p]
         gath[mx, p : p + 1, :] = packs[p]
 
-    for p in range(1, nx):
+    for peer in peers(True):
         pltpu.make_async_remote_copy(
             src_ref=msg,
             dst_ref=gath.at[mx],
             send_sem=sum_send,
             recv_sem=sum_recv,
-            device_id=(lax.rem(mx + p, nx), my),
+            device_id=(peer, my),
             device_id_type=MESH,
         ).start()
 
@@ -471,7 +512,6 @@
             pltpu.VMEM((10, 6, 2, 72, HALF), F32),
             pltpu.VMEM((10, 6, 2, 72, HALF), F32),
             pltpu.VMEM((10, 3, 2, 88, HALF), F32),
-            pltpu.VMEM((10, 3, 2, 72, HALF), F32),
             pltpu.VMEM((10, 2, 72, HALF), F32),
             pltpu.VMEM((XL, YL, ZL), F32),
             pltpu.VMEM((2, 72, HALF), F32),

time: 22.7 us -> 22.4 us (0.987)
  the two profiles are of different devices: /device:TPU:9 before, /device:TPU:1 now
where the time goes in v4:
time: 22.4 us; the launch traced here: 22 us
  Pallas kernels  21.3 us (95%)
  between operations  0.64 us (3%)
    pallas_call x1, Pallas kernels, local(): pl.pallas_call(functools.partial(main_kernel, nx, ny), out_shape=(pltpu.V...  20.5 us
    pallas_call x1, Pallas kernels, local(): pl.pallas_call(store_kernel, out_shape=(jax.ShapeDtypeStruct((1, YL), F32...  0.81 us

profile of v4, /device:TPU:1, one launch (start us, length us, event | category | flops | bytes accessed | tf_op | source)
XLA Modules:
  0.0 22.0 jit_solution(5507627741575345681)
XLA Ops:
  0.6 20.5 %germano.1 = (f32[1,64]{1,0:T(1,128)S(1)}, f32[8,64,256]{2,1,0:T(8,128)S(1)}) custom-call(f32[3,8,64,256]{3,2,1,0:T(8,128)} %vel.1), custom_call_target="tpu_custom_call" | custom-call | tf_op jit(solution)/shard_map/germano/pallas_call | solution.py:499
  21.2 0.8 %store.1 = (f32[1,64]{1,0:T(1,128)}, f32[8,64,256]{2,1,0:T(8,128)}) custom-call(f32[1,64]{1,0:T(1,128)S(1)} %get-tuple-element.6.coefficient, f32[8,64,256]{2,1,0:T(8,128)S(1)} %get-tuple-element.7.viscosity), custom_call_target="tpu_custom_call" | custom-call | tf_op jit(solution)/shard_map/store/pallas_call | solution.py:537

commit v5 on v4

--- a/solution.py
+++ b/solution.py
@@ -14,6 +14,8 @@
 YL = 64
 ZL = 256
 HALF = 128
+NEAR = (1, -1, 2, -2, 8, -8)
+FAR = (8, -8, 16)
 CUTS = (0, 24, 48, 56, 64)
 CHUNKS = len(CUTS) - 1
 clip_high = 0.1
@@ -160,7 +162,7 @@
     vel, coefficient, viscosity,
     nat, w, zu, dz, zp, zs, vf, sr, strength, acc, msg, gath, order,
     in_sem, slow_send, slow_recv, fast_send, fast_recv, wall_send, wall_recv,
-    corner_send, corner_recv, sum_send, sum_recv,
+    corner_send, corner_recv, sum_send, sum_recv, round_sem,
 ):
     mx = lax.axis_index("gx")
     my = lax.axis_index("gy")
@@ -188,19 +190,19 @@
     def signal(sem, x, y):
         pl.semaphore_signal(sem, inc=1, device_id=(x, y), device_id_type=MESH)
 
+    def along(step):
+        return lax.rem(mx + (step + nx), nx)
+
     barrier = pltpu.get_barrier_semaphore()
+    for step in NEAR:
+        signal(barrier, along(step), my)
+    pl.when(has_low)(lambda: signal(barrier, mx, my - 1))
+    pl.when(has_high)(lambda: signal(barrier, mx, my + 1))
     loads = []
     for g, q in enumerate((8, 6, 4, 2)):
         cells = pl.ds(base(q) - 2, 2)
         loads.append(pltpu.make_async_copy(vel.at[:, cells], nat.at[:, cells], in_sem.at[g]))
-        if g == 0:
-            loads[g].start()
-    for peer in peers(True):
-        signal(barrier, peer, my)
-    pl.when(has_low)(lambda: signal(barrier, mx, my - 1))
-    pl.when(has_high)(lambda: signal(barrier, mx, my + 1))
-    for load in loads[1:]:
-        load.start()
+        loads[g].start()
 
     def clear(first, count):
         def body(x):
@@ -295,18 +297,18 @@
     inner = range(1, 8)
     px, pz = mx // 8, lax.rem(mx, 8) // 2
     either, both = jnp.logical_or, jnp.logical_and
-    first = either(pz == 0, both(pz == 1, px < 2))
-    second = either(
-        both(pz == 1, px >= 2), either(both(pz == 2, px < 2), both(pz == 3, px == 0))
-    )
+    first = pz == 0
+    second = both(px == 0, pz > 0)
     third = jnp.logical_not(either(first, second))
 
     def meet():
         pl.semaphore_wait(
-            barrier, nx - 1 + has_low.astype(jnp.int32) + has_high.astype(jnp.int32)
+            barrier, len(NEAR) + has_low.astype(jnp.int32) + has_high.astype(jnp.int32)
         )
         for copy in slow_copies:
             copy.start()
+        for step in NEAR:
+            signal(round_sem.at[0], along(step), my)
 
     def send_near():
         pl.when(has_low)(to_low.start)
@@ -345,6 +347,10 @@
     spans(0, inner, (False, True))
     strains(1, inner)
     sums(2, range(2, 7))
+
+    pl.semaphore_wait(round_sem.at[0], len(NEAR))
+    for step in FAR:
+        signal(round_sem.at[1], along(step), my)
 
     @pl.when(has_low)
     def _():
@@ -397,6 +403,7 @@
         msg[p : p + 1, :] = packs[p]
         gath[mx, p : p + 1, :] = packs[p]
 
+    pl.semaphore_wait(round_sem.at[1], len(FAR))
     for peer in peers(True):
         pltpu.make_async_remote_copy(
             src_ref=msg,
@@ -529,6 +536,7 @@
             dma((4,)),
             dma,
             dma,
+            pltpu.SemaphoreType.REGULAR((2,)),
         ],
         compiler_params=pltpu.CompilerParams(collective_id=0, has_side_effects=True),
         name="germano",

time: 22.4 us -> 22.1 us (0.987)
  Pallas kernels: 21.3 us -> 21 us
    pallas_call x1, Pallas kernels: 20.5 us -> 20.2 us  [local(): pl.pallas_call(functools.partial(main_kernel, nx, ny), out_shape=(pltpu.V...]
where the time goes in v5:
time: 22.1 us; the launch traced here: 21.7 us
  Pallas kernels  21 us (95%)
  between operations  0.64 us (3%)
    pallas_call x1, Pallas kernels, local(): pl.pallas_call(functools.partial(main_kernel, nx, ny), out_shape=(pltpu.V...  20.2 us
    pallas_call x1, Pallas kernels, local(): pl.pallas_call(store_kernel, out_shape=(jax.ShapeDtypeStruct((1, YL), F32...  0.81 us

profile of v5, /device:TPU:1, one launch (start us, length us, event | category | flops | bytes accessed | tf_op | source)
XLA Modules:
  0.0 21.7 jit_solution(2344644772541915114)
XLA Ops:
  0.6 20.2 %germano.1 = (f32[1,64]{1,0:T(1,128)S(1)}, f32[8,64,256]{2,1,0:T(8,128)S(1)}) custom-call(f32[3,8,64,256]{3,2,1,0:T(8,128)} %vel.1), custom_call_target="tpu_custom_call" | custom-call | tf_op jit(solution)/shard_map/germano/pallas_call | solution.py:506
  20.9 0.8 %store.1 = (f32[1,64]{1,0:T(1,128)}, f32[8,64,256]{2,1,0:T(8,128)}) custom-call(f32[1,64]{1,0:T(1,128)S(1)} %get-tuple-element.6.coefficient, f32[8,64,256]{2,1,0:T(8,128)S(1)} %get-tuple-element.7.viscosity), custom_call_target="tpu_custom_call" | custom-call | tf_op jit(solution)/shard_map/store/pallas_call | solution.py:545

commit v6 on v5

--- a/solution.py
+++ b/solution.py
@@ -376,20 +376,19 @@
     strains(1, (0, 8))
     sums(2, (0, 1, 7, 8))
 
-    done_strains = done_sums = 0
+    done_strains, done_sums = 1, 2
     for c, copy in enumerate(slow_copies):
-        last = c == len(slow_copies) - 1
         copy.wait_recv()
-        if c == 0:
-            pl.when(has_low)(corners[0].wait_recv)
-        if last:
-            pl.when(has_high)(corners[1].wait_recv)
-        ready_strains = 9 if last else (CUTS[c + 1] + 1) // 8
-        ready_sums = 9 if last else ready_strains - 1
+        ready_strains = (CUTS[c + 1] + 1) // 8
         spans(10, range(done_strains, ready_strains), (True, False))
         strains(9, range(done_strains, ready_strains))
-        sums(8, range(done_sums, ready_sums))
-        done_strains, done_sums = ready_strains, ready_sums
+        sums(8, range(done_sums, ready_strains - 1))
+        done_strains, done_sums = ready_strains, ready_strains - 1
+    pl.when(has_low)(corners[0].wait_recv)
+    pl.when(has_high)(corners[1].wait_recv)
+    spans(10, (0, 8), (True, False))
+    strains(9, (0, 8))
+    sums(8, (0, 1, 7, 8))
 
     packs = []
     for p in range(2):

time: 22.1 us -> 22.1 us (level); the launches traced: 21.7 us -> 21.9 us
  Pallas kernels: 21 us -> 21.3 us
    pallas_call x1, Pallas kernels: 20.2 us -> 20.5 us  [local(): pl.pallas_call(functools.partial(main_kernel, nx, ny), out_shape=(pltpu.V...]
where the time goes in v6:
time: 22.1 us; the launch traced here: 21.9 us
  Pallas kernels  21.3 us (96%)
  between operations  0.64 us (3%)
    pallas_call x1, Pallas kernels, local(): pl.pallas_call(functools.partial(main_kernel, nx, ny), out_shape=(pltpu.V...  20.5 us
    pallas_call x1, Pallas kernels, local(): pl.pallas_call(store_kernel, out_shape=(jax.ShapeDtypeStruct((1, YL), F32...  0.81 us

profile of v6, /device:TPU:1, one launch (start us, length us, event | category | flops | bytes accessed | tf_op | source)
XLA Modules:
  0.0 21.9 jit_solution(14404327951062378516)
XLA Ops:
  0.6 20.5 %germano.1 = (f32[1,64]{1,0:T(1,128)S(1)}, f32[8,64,256]{2,1,0:T(8,128)S(1)}) custom-call(f32[3,8,64,256]{3,2,1,0:T(8,128)} %vel.1), custom_call_target="tpu_custom_call" | custom-call | tf_op jit(solution)/shard_map/germano/pallas_call | solution.py:505
  21.1 0.8 %store.1 = (f32[1,64]{1,0:T(1,128)}, f32[8,64,256]{2,1,0:T(8,128)}) custom-call(f32[1,64]{1,0:T(1,128)S(1)} %get-tuple-element.6.coefficient, f32[8,64,256]{2,1,0:T(8,128)S(1)} %get-tuple-element.7.viscosity), custom_call_target="tpu_custom_call" | custom-call | tf_op jit(solution)/shard_map/store/pallas_call | solution.py:544
